TPU v7x, 32 devices: a whole 2x2x4 slice. The times are simulated.
32 devices in a mesh: space: 16 (over z, y, x), level: 2 (over core).
Axes of the slice: x: 2, y: 2, z: 4, core: 2. Of those that a mesh axis runs over, the one named last changes fastest.
Arguments:
- velocity: float32 [2, 16, 16384], P(None, 'level', 'space'), may hold values from -3 to 3
- density: float32 [16, 16384], P('level', 'space'), may hold values from -6 to 6
- elevation: float32 [16384], P('space'), may hold values from -3 to 3
- grad_weights: float32 [2, 6, 16384], P(None, None, 'space'), may hold values from -2.4 to 2.4
- lap_weights: float32 [6, 16384], P(None, 'space'), may hold values from 0.02 to 0.2
- coriolis: float32 [16384], P('space'), may hold values from 0.5 to 2
- node_area: float32 [16384], P('space'), may hold values from 1 to 100, as said below
- thickness: float32 [16], P('level'), may hold values from 0.5 to 2
- send_list: int32 [16, 256], P('space'), may hold values from 0 to 1023
- neighbours: int32 [6, 16384], P(None, 'space'), may hold values from 0 to 1279
- bottom: int32 [16384], P('space'), may hold values from 0 to 16, as said below
Outputs:
- velocity_out: float32 [2, 16, 16384], P(None, 'level', 'space')
- density_out: float32 [16, 16384], P('level', 'space')
- elevation_out: float32 [16384], P('space')
- volume_drift: float32 [4], replicated
Inputs may be any that keep to these rules, and one draw needn't show every extreme that they name: `send_list`: local node numbers within the sending partition; the first 128 go to the partition one below along space, the other 128 to the one above. `neighbours`: slots below 1024 are the partition's own nodes; the next 128 are halo slots filled from the partition below, the last 128 from the partition above. Levels of a node are wet from the surface down to bottom - 1; a node with 0 is dry. Some partitions are shallower than others. `node_area`: positive areas.
All inputs are finite; a program needn't handle non-finite values.
Results may differ from a plain program's by a relative error of at most 0.00013.
Values sent between devices are 32-bit elements; how exact they have to be, the bound alone decides.
A program may use at most 64 MiB of HBM per device.

v0:
```python
import functools

import jax
import jax.numpy as jnp
from jax import lax
from jax.experimental import pallas as pl
from jax.experimental.pallas import tpu as pltpu
from jax.sharding import PartitionSpec as P

STEPS = 4
LANES = 128

time_step = 0.1
buoyancy = 0.5
drag_rate = 0.5


def lane_gather(values, lanes):
    return jnp.take_along_axis(values, lanes, axis=1, mode="promise_in_bounds")


def pick(tiles, lanes, masks):
    found = lane_gather(tiles[0], lanes)
    for tile, mask in zip(tiles[1:], masks):
        found = jnp.where(mask, lane_gather(tile, lanes), found)
    return found


def running_sum(values, rows, row_ids):
    shift = 1
    while shift < rows:
        moved = pltpu.roll(values, shift, 0)
        values = values + jnp.where(row_ids >= shift, moved, 0.0)
        shift *= 2
    return values


def spread_sum(values):
    shift = values.shape[0] // 2
    while shift:
        values = values + pltpu.roll(values, shift, 0)
        shift //= 2
    return values


def kernel(
    n_space, n_level, width, rows, blocks, near_count,
    vel, den, ele, grad, lap, cor, area, thick, send, near, bot,
    vel_out, den_out, ele_out, drift_out,
    own, eta, lanes_of, block_of, weight_of, q_lanes, q_block, q_weight,
    part, q_part, q_of, q_sum, small, out, out_small, halo, halo_small, peer_out, peer,
    vol, vol_line, vol_all,
    main_send, main_recv, hs_send, hs_recv, peer_send, peer_recv, vol_send, vol_recv, column_in,
    load_sem, thick_in, *loaded,
):
    sp = lax.axis_index("space")
    lv = lax.axis_index("level")
    n_dev = n_space * n_level
    has = (sp > 0, sp < n_space - 1)
    ends = (sp - 1, sp + 1)
    low = jnp.where(has[0], 1, 0)
    high = jnp.where(has[1], 1, 0)
    others = [lax.rem(lv + d, n_level) for d in range(1, n_level)]

    barrier = pltpu.get_barrier_semaphore()

    mine, place = sp // width, lax.rem(sp, width)
    column = [(lax.rem(sp + d * width, n_space), lv) for d in range(1, n_space // width)]
    row = [(mine * width + lax.rem(place + d, width), lax.rem(lv + e, n_level))
           for d in range(width) for e in range(n_level) if d or e]
    for q, level in row + column:
        pl.semaphore_signal(barrier, inc=1, device_id={"space": q, "level": level})
    for side in range(2):
        @pl.when(has[side])
        def _():
            for q in [lv] + others:
                pl.semaphore_signal(barrier, inc=1, device_id={"space": ends[side], "level": q})

    loads = [
        pltpu.make_async_copy(ref, buffer, load_sem.at[i])
        for i, (ref, buffer) in enumerate(zip(
            (vel, den, ele, grad, lap, cor, area, thick, send, near, bot),
            loaded[:7] + (thick_in,) + loaded[7:]))
    ]
    for load in loads:
        load.start()

    row_ids = lax.broadcasted_iota(jnp.int32, (rows, LANES), 0)
    eight = lax.broadcasted_iota(jnp.int32, (8, LANES), 0)
    odd = jnp.bitwise_and(eight, 1) == 1
    lane_ids = lax.broadcasted_iota(jnp.int32, (1, LANES), 1)
    level_ids = row_ids + lv * rows

    def wide(row, count=rows):
        return jnp.broadcast_to(row, (count, LANES))

    for side in range(2):
        @pl.when(jnp.logical_not(has[side]))
        def _():
            halo[:, side] = jnp.zeros(halo.shape[:1] + halo.shape[2:], jnp.float32)
            halo_small[:, side] = jnp.zeros(halo_small.shape[:1] + halo_small.shape[2:], jnp.float32)

    for load in loads:
        load.wait()
    vel, den, ele, grad, lap, cor, area, send, near, bot = loaded

    thickness = jnp.zeros((rows, LANES), jnp.float32)
    for r in range(rows):
        thickness = jnp.where(row_ids == r, thick_in[r], thickness)

    def prepare(t, _):
        here = pl.ds(pl.multiple_of(t * LANES, LANES), LANES)
        wet = level_ids < wide(bot[pl.ds(t, 1), :])
        own[0, t] = jnp.where(wet, vel[0, :, here], 0.0)
        own[1, t] = jnp.where(wet, vel[1, :, here], 0.0)
        own[2, t] = den[:, here]
        eta[t] = jnp.where(lv == 0, wide(ele[pl.ds(t, 1), :], 8), 0.0)
        lane_pack = jnp.zeros((8, LANES), jnp.int32)
        block_pack = jnp.zeros((8, LANES), jnp.int32)
        packs = [jnp.zeros((8, LANES), jnp.float32) for _ in range(4)]
        for k in range(near_count):
            slot = wide(near[k:k + 1, here])
            block = lax.shift_right_logical(slot, 7)
            lanes = jnp.bitwise_and(slot, LANES - 1)
            inside = block < blocks
            outside = jnp.where(inside, 0, jnp.where(block == blocks, low, high)) > 0
            lanes_of[t, k] = lanes
            block_of[t, k] = block
            values = (wide(grad[k, 0:1, here]), wide(grad[k, 1:2, here]), wide(lap[k:k + 1, here]))
            picked = [jnp.where(mask, value, 0.0) for mask in (inside, outside) for value in values]
            for i in range(6):
                weight_of[t, k, i] = picked[i]
            mine = eight == k
            lane_pack = jnp.where(mine, lanes[:8], lane_pack)
            block_pack = jnp.where(mine, block[:8], block_pack)
            packs = [jnp.where(mine, picked[i][:8], pack) for i, pack in zip((0, 1, 3, 4), packs)]
        q_lanes[t] = lane_pack
        q_block[t] = block_pack
        for i in range(4):
            q_weight[t, i] = packs[i]
        return 0

    lax.fori_loop(0, blocks, prepare, 0)
    wet_area = area[...] * jnp.where(bot[...] > 0, 1.0, 0.0)
    count = jnp.where(lv == 0, 1.0, 0.0)
    vol[...] = jnp.where(eight == STEPS, wide(jnp.sum(wet_area, axis=0, keepdims=True), 8) * count, 0.0)

    def version(q):
        return jnp.where(q > lv, 1, 0)

    def main_copy(s, side):
        return pltpu.make_async_remote_copy(
            src_ref=out.at[s, side], dst_ref=halo.at[s, 1 - side],
            send_sem=main_send.at[s, side], recv_sem=main_recv.at[s, 1 - side],
            device_id={"space": ends[side], "level": lv}, device_id_type=pl.DeviceIdType.MESH)

    def small_copy(s, side, q, slot):
        return pltpu.make_async_remote_copy(
            src_ref=out_small.at[s, side, version(q)], dst_ref=halo_small.at[s, 1 - side, slot],
            send_sem=hs_send.at[s, side, q], recv_sem=hs_recv.at[s, 1 - side, slot],
            device_id={"space": ends[side], "level": q}, device_id_type=pl.DeviceIdType.MESH)

    def peer_copy(s, q, slot):
        return pltpu.make_async_remote_copy(
            src_ref=peer_out.at[s, jnp.where(s < STEPS, version(q), 0)], dst_ref=peer.at[s, slot],
            send_sem=peer_send.at[s, q], recv_sem=peer_recv.at[s, slot],
            device_id={"space": sp, "level": q}, device_id_type=pl.DeviceIdType.MESH)

    dev = sp * n_level + lv

    def vol_copy(q, slot):
        return pltpu.make_async_remote_copy(
            src_ref=vol_line, dst_ref=vol_all.at[slot],
            send_sem=vol_send.at[q], recv_sem=vol_recv.at[slot],
            device_id={"space": q // n_level, "level": lax.rem(q, n_level)},
            device_id_type=pl.DeviceIdType.MESH)

    def scalars(t, rho, level):
        heavy = level + buoyancy * spread_sum(rho * thickness)
        small[t] = jnp.where(odd, heavy, level)
        return heavy

    def stage_out(s):
        for side in range(2):
            slot = wide(send[:, side * LANES:(side + 1) * LANES])
            lanes = jnp.bitwise_and(slot, LANES - 1)
            block = lax.shift_right_logical(slot, 7)
            masks = [block == b for b in range(1, blocks)]
            for g in range(3):
                out[s, side, g * rows:(g + 1) * rows] = pick([own[g, b] for b in range(blocks)], lanes, masks)
            found = pick([small[b] for b in range(blocks)], lanes[:8], [m[:8] for m in masks])
            out[s, side, 3 * rows:3 * rows + 8] = found
            for i in range(2):
                out_small[s, side, i] = found[i:i + 1]

    def send_out(s):
        for side in range(2):
            @pl.when(has[side])
            def _():
                main_copy(s, side).start()
                for q in others:
                    small_copy(s, side, q, lv).start()
        for q in others:
            peer_copy(s, q, lv).start()

    def close(s):
        for q in others:
            peer_copy(s, q, lv).wait_send()
        for side in range(2):
            @pl.when(has[side])
            def _():
                main_copy(s, side).wait_send()
                for q in others:
                    small_copy(s, side, q, lv).wait_send()

    def own_parts():
        def body(t, _):
            tiles = [[own[g, b] for b in range(blocks)] for g in range(3)]
            here = [own[g, t] for g in range(3)]
            zero = jnp.zeros((rows, LANES), jnp.float32)
            sums = [zero] * 6
            for k in range(near_count):
                block = block_of[t, k]
                masks = [block == b for b in range(1, blocks)]
                diff = [pick(tiles[g], lanes_of[t, k], masks) - here[g] for g in range(3)]
                sums = gathered(sums, diff, [weight_of[t, k, i] for i in range(3)])
            for i in range(6):
                part[t, i] = sums[i]
            return 0
        lax.fori_loop(0, blocks, body, 0)

    def gathered(sums, diff, weights):
        east, north, smooth = weights
        return [sums[0] + smooth * diff[0], sums[1] + smooth * diff[1], sums[2] + smooth * diff[2],
                sums[3] + east * diff[2], sums[4] + north * diff[2],
                sums[5] + (east * diff[0] + north * diff[1])]

    def own_surface(s):
        total = peer_out[s, 0]
        for q in others:
            total = total + peer[s, q]
        q_sum[...] = total
        for t in range(blocks):
            q_of[t] = wide(q_sum[t:t + 1, :], 8)
        tiles = [q_of[b] for b in range(blocks)]
        for t in range(blocks):
            block = q_block[t]
            diff = pick(tiles, q_lanes[t], [block == b for b in range(1, blocks)]) - tiles[t]
            q_part[t, 0] = q_weight[t, 0] * diff
            q_part[t, 1] = q_weight[t, 1] * diff

    def receive(s):
        for side in range(2):
            @pl.when(has[side])
            def _():
                main_copy(s, 1 - side).wait_recv()
                for q in others:
                    small_copy(s, 1 - side, q, q).wait_recv()
        for side in range(2):
            total = halo[s, side, 3 * rows:3 * rows + 1]
            for q in others:
                total = total + halo_small[s, side, q]
            q_of[blocks + side] = wide(total, 8)

    def finish(s):
        edges = [[halo[s, side, g * rows:(g + 1) * rows] for side in range(2)] for g in range(3)]
        edges.append([q_of[blocks], q_of[blocks + 1]])

        def body(t, carry):
            volume, light, heavy = carry
            here = [own[g, t] for g in range(3)]
            sums = [part[t, i] for i in range(6)]
            for k in range(near_count):
                lanes = lanes_of[t, k]
                upper = block_of[t, k] == blocks + 1
                diff = [jnp.where(upper, lane_gather(edges[g][1], lanes), lane_gather(edges[g][0], lanes)) - here[g]
                        for g in range(3)]
                sums = gathered(sums, diff, [weight_of[t, k, 3 + i] for i in range(3)])
            lap0, lap1, lap2, east2, north2, flow = sums
            lanes = q_lanes[t]
            diff = jnp.where(q_block[t] == blocks + 1, lane_gather(edges[3][1], lanes),
                             lane_gather(edges[3][0], lanes)) - q_of[t]
            slope0 = spread_sum(q_part[t, 0] + q_weight[t, 2] * diff)
            slope1 = spread_sum(q_part[t, 1] + q_weight[t, 3] * diff)
            bottom = wide(bot[pl.ds(t, 1), :])
            turn = wide(cor[pl.ds(t, 1), :])
            drag = jnp.where(level_ids == bottom - 1, drag_rate, 0.0)
            u, v, rho = here
            east3, north3 = thickness * east2, thickness * north2
            east3 = slope0 + buoyancy * (running_sum(east3, rows, row_ids) - 0.5 * east3)
            north3 = slope1 + buoyancy * (running_sum(north3, rows, row_ids) - 0.5 * north3)
            push0 = -east3 + turn * v + lap0 - drag * u
            push1 = -north3 - turn * u + lap1 - drag * v
            wet = level_ids < bottom
            own[0, t] = jnp.where(wet, u + time_step * push0, 0.0)
            own[1, t] = jnp.where(wet, v + time_step * push1, 0.0)
            fresh = rho + time_step * (lap2 - u * east2 - v * north2)
            own[2, t] = fresh
            diverge = jnp.where(bottom[:8] > 0, spread_sum(thickness * flow), 0.0)
            level = eta[t] - time_step * diverge
            eta[t] = level
            dense = scalars(t, fresh, level)
            return (volume + wide(area[pl.ds(t, 1), :], 8) * diverge,
                    jnp.where(eight == t, level, light), jnp.where(eight == t, dense, heavy))

        zero = jnp.zeros((8, LANES), jnp.float32)
        volume, light, heavy = lax.fori_loop(0, blocks, body, (zero, zero, zero), unroll=True)
        vol[...] = jnp.where(eight == s, volume, vol[...])
        peer_out[s + 1, 0] = light
        peer_out[s + 1, 1] = heavy

    def first(t, carry):
        light, heavy = carry
        dense = scalars(t, own[2, t], eta[t])
        return jnp.where(eight == t, eta[t], light), jnp.where(eight == t, dense, heavy)

    zero = jnp.zeros((8, LANES), jnp.float32)
    light, heavy = lax.fori_loop(0, blocks, first, (zero, zero), unroll=True)
    peer_out[0, 0] = light
    peer_out[0, 1] = heavy
    stage_out(0)

    expected = len(row) + len(column) + n_level * (low + high)
    pl.semaphore_wait(barrier, expected)
    for q, level in row:
        pl.semaphore_signal(column_in, inc=1, device_id={"space": q, "level": level})

    def step(s, _):
        send_out(s)
        own_parts()
        for q in others:
            peer_copy(s, q, q).wait_recv()
        own_surface(s)
        receive(s)
        finish(s)

        @pl.when(s < STEPS - 1)
        def _():
            stage_out(s + 1)

        close(s)
        return 0

    lax.fori_loop(0, STEPS, step, 0)

    sums = jnp.sum(vol[...], axis=1, keepdims=True)
    line = jnp.zeros((1, LANES), jnp.float32)
    for i in range(STEPS + 1):
        line = jnp.where(lane_ids == i, sums[i:i + 1], line)
    vol_line[...] = line
    pl.semaphore_wait(column_in, len(row))
    for q in others:
        peer_copy(STEPS, q, lv).start()

    def start(d, _):
        vol_copy(lax.rem(dev + d, n_dev), dev).start()
        return 0

    lax.fori_loop(1, n_dev, start, 0)

    for t in range(blocks):
        here = slice(t * LANES, (t + 1) * LANES)
        vel_out[0, :, here] = own[0, t]
        vel_out[1, :, here] = own[1, t]
        den_out[:, here] = own[2, t]

    level = peer_out[STEPS, 0]
    for q in others:
        peer_copy(STEPS, q, q).wait_recv()
        level = level + peer[STEPS, q]

    def collect(d, total):
        q = lax.rem(dev + d, n_dev)
        vol_copy(q, q).wait_recv()
        return total + vol_all[q]

    total = lax.fori_loop(1, n_dev, collect, vol_line[...])
    drifts = total / total[:, STEPS:STEPS + 1]
    shift = jnp.sum(jnp.where(lane_ids < STEPS, drifts, 0.0), axis=1, keepdims=True)
    ele_out[...] = level + time_step * shift
    drift_out[...] = drifts
    for q in others:
        peer_copy(STEPS, q, lv).wait_send()

    def done(d, _):
        vol_copy(lax.rem(dev + d, n_dev), dev).wait_send()
        return 0

    lax.fori_loop(1, n_dev, done, 0)


def emit(vel, den, ele, drift, vel_out, den_out, ele_out, drift_out):
    vel_out[...] = vel[...]
    den_out[...] = den[...]
    ele_out[...] = ele[...]
    drift_out[...] = drift[:, :STEPS]


def solution(mesh):
    n_space, n_level = mesh.shape["space"], mesh.shape["level"]
    n_dev = n_space * n_level
    width = max(w for w in range(1, n_space + 1) if n_space % w == 0 and w * w <= n_space)

    def local(velocity, density, elevation, grad_weights, lap_weights, coriolis,
              node_area, thickness, send_list, neighbours, bottom):
        rows, nodes = density.shape
        blocks = nodes // LANES
        near_count = neighbours.shape[0]
        f32, i32 = jnp.float32, jnp.int32
        plane = (blocks, LANES)
        vmem = pl.BlockSpec(memory_space=pltpu.VMEM)
        hbm = pl.BlockSpec(memory_space=pltpu.HBM)
        dma = pltpu.SemaphoreType.DMA
        tile = (rows, LANES)
        pack = (8, LANES)
        arrays = [velocity, density, elevation.reshape(plane), grad_weights.transpose(1, 0, 2), lap_weights,
                  coriolis.reshape(plane), node_area.reshape(plane), thickness, send_list,
                  neighbours, bottom.reshape(plane)]
        arrays = [pltpu.with_memory_space_constraint(a, pltpu.HBM) for a in arrays]
        out = pl.pallas_call(
            functools.partial(kernel, n_space, n_level, width, rows, blocks, near_count),
            out_shape=(
                jax.ShapeDtypeStruct(velocity.shape, f32),
                jax.ShapeDtypeStruct(density.shape, f32),
                jax.ShapeDtypeStruct(plane, f32),
                jax.ShapeDtypeStruct((1, LANES), f32),
            ),
            in_specs=[hbm] * 11,
            out_specs=(vmem, vmem, vmem, vmem),
            scratch_shapes=[
                pltpu.VMEM((3, blocks) + tile, f32),
                pltpu.VMEM((blocks,) + pack, f32),
                pltpu.VMEM((blocks, near_count) + tile, i32),
                pltpu.VMEM((blocks, near_count) + tile, i32),
                pltpu.VMEM((blocks, near_count, 6) + tile, f32),
                pltpu.VMEM((blocks,) + pack, i32),
                pltpu.VMEM((blocks,) + pack, i32),
                pltpu.VMEM((blocks, 4) + pack, f32),
                pltpu.VMEM((blocks, 6) + tile, f32),
                pltpu.VMEM((blocks, 2) + pack, f32),
                pltpu.VMEM((blocks + 2,) + pack, f32),
                pltpu.VMEM(plane, f32),
                pltpu.VMEM((blocks,) + pack, f32),
                pltpu.VMEM((STEPS, 2, 3 * rows + 8, LANES), f32),
                pltpu.VMEM((STEPS, 2, 2, 1, LANES), f32),
                pltpu.VMEM((STEPS, 2, 3 * rows + 8, LANES), f32),
                pltpu.VMEM((STEPS, 2, n_level, 1, LANES), f32),
                pltpu.VMEM((STEPS + 1, 2) + plane, f32),
                pltpu.VMEM((STEPS + 1, n_level) + plane, f32),
                pltpu.VMEM(pack, f32),
                pltpu.VMEM((1, LANES), f32),
                pltpu.VMEM((n_dev, 1, LANES), f32),
                dma((STEPS, 2)), dma((STEPS, 2)),
                dma((STEPS, 2, n_level)), dma((STEPS, 2, n_level)),
                dma((STEPS + 1, n_level)), dma((STEPS + 1, n_level)),
                dma((n_dev,)), dma((n_dev,)),
                pltpu.SemaphoreType.REGULAR,
                dma((11,)),
                pltpu.SMEM(thickness.shape, f32),
            ] + [pltpu.VMEM(a.shape, a.dtype) for a in arrays[:7] + arrays[8:]],
            compiler_params=pltpu.CompilerParams(
                collective_id=0, has_side_effects=True, vmem_limit_bytes=16 * 2 ** 20),
        )(*arrays)
        out = pl.pallas_call(
            emit,
            out_shape=(
                jax.ShapeDtypeStruct(velocity.shape, f32),
                jax.ShapeDtypeStruct(density.shape, f32),
                jax.ShapeDtypeStruct(plane, f32),
                jax.ShapeDtypeStruct((1, STEPS), f32),
            ),
            in_specs=[vmem] * 4,
            out_specs=(vmem,) * 4,
            compiler_params=pltpu.CompilerParams(vmem_limit_bytes=2 ** 20),
        )(*out)
        return out[0], out[1], out[2].reshape(nodes), out[3].reshape(STEPS)

    return jax.shard_map(
        local,
        mesh=mesh,
        in_specs=(
            P(None, "level", "space"),
            P("level", "space"),
            P("space"),
            P(None, None, "space"),
            P(None, "space"),
            P("space"),
            P("space"),
            P("level"),
            P("space", None),
            P(None, "space"),
            P("space"),
        ),
        out_specs=(P(None, "level", "space"), P("level", "space"), P("space"), P()),
        check_vma=False,
    )
```

profile of v0, /device:TPU:0, one launch (start us, length us, event | category | flops | bytes accessed | tf_op | source)
XLA Modules:
  0.0 30.4 jit_solution(752815413004146149)
XLA Ops:
  0.6 29.1 %shard_map.138 = (f32[2,8,1024]{2,1,0:T(8,128)S(1)}, f32[8,1024]{1,0:T(8,128)S(1)}, f32[8,128]{1,0:T(8,128)S(1)}, f32[1,128]{1,0:T(1,128)S(1)}) custom-call(f32[2,8,1024]{2,1,0:T(8,128)} %vel.1, f32[8,1024]{1,0:T(8,128)} %den.1, f32[8,128]{1,0:T(8,128)} %bitcast.8, f32[6,2,1024]{2,1,0:T(2,128)} %bitcast.7, f32[6,1024]{1,0:T(8,128)} %lap.1, ...), custom_call_target="tpu_custom_call" | custom-call | tf_op jit(solution)/shard_map/pallas_call | solution.py:420
  29.7 0.6 %shard_map.139 = (f32[2,8,1024]{2,1,0:T(8,128)}, f32[8,1024]{1,0:T(8,128)}, f32[8,128]{1,0:T(8,128)}, f32[1,4]{1,0:T(1,128)}) custom-call(f32[2,8,1024]{2,1,0:T(8,128)S(1)} %get-tuple-element.12.vel, f32[8,1024]{1,0:T(8,128)S(1)} %get-tuple-element.13.den, f32[8,128]{1,0:T(8,128)S(1)} %get-tuple-element.14.ele, f32[1,128]{1,0:T(1,128)S(1)} %get-tuple-element.15.drift), custom_call_target="tpu_custom_call" | custom-call | tf_op jit(solution)/shard_map/pallas_call | solution.py:464
where the time goes:
time: 30.5 us; the launch traced here: 30.4 us
  Pallas kernels  29.7 us (97%)
  between operations  0.64 us (2%)
    pallas_call x1, Pallas kernels, local(): pl.pallas_call(functools.partial(kernel, n_space, n_level, width, rows, b...  29.1 us
    pallas_call x1, Pallas kernels, local(): pl.pallas_call(emit, out_shape=(jax.ShapeDtypeStruct(velocity.shape, f32)...  0.65 us

commit v1 on v0

--- a/solution.py
+++ b/solution.py
@@ -47,20 +47,23 @@
     n_space, n_level, width, rows, blocks, near_count,
     vel, den, ele, grad, lap, cor, area, thick, send, near, bot,
     vel_out, den_out, ele_out, drift_out,
-    own, eta, lanes_of, block_of, weight_of, q_lanes, q_block, q_weight,
-    part, q_part, q_of, q_sum, small, out, out_small, halo, halo_small, peer_out, peer,
-    vol, vol_line, vol_all,
-    main_send, main_recv, hs_send, hs_recv, peer_send, peer_recv, vol_send, vol_recv, column_in,
+    own, eta, cor_of, bot_of, lanes_of, block_of, weight_of, pack_lanes, pack_block, pack_weight,
+    flow_lanes, flow_block, flow_own, flow_halo,
+    part, q_part, q_of, q_edge, q_sum, small, out, out_small, halo, halo_small, peer_out, peer,
+    vol, vol_line, vol_all, adjoint, adjoint_in,
+    main_send, main_recv, hs_send, hs_recv, peer_send, peer_recv, vol_send, vol_recv, adj_send, adj_recv, column_in,
     load_sem, thick_in, *loaded,
 ):
     sp = lax.axis_index("space")
     lv = lax.axis_index("level")
     n_dev = n_space * n_level
+    dev = sp * n_level + lv
     has = (sp > 0, sp < n_space - 1)
     ends = (sp - 1, sp + 1)
     low = jnp.where(has[0], 1, 0)
     high = jnp.where(has[1], 1, 0)
     others = [lax.rem(lv + d, n_level) for d in range(1, n_level)]
+    targets = blocks + 2
 
     barrier = pltpu.get_barrier_semaphore()
 
@@ -99,6 +102,7 @@
         def _():
             halo[:, side] = jnp.zeros(halo.shape[:1] + halo.shape[2:], jnp.float32)
             halo_small[:, side] = jnp.zeros(halo_small.shape[:1] + halo_small.shape[2:], jnp.float32)
+            adjoint_in[side] = jnp.zeros(adjoint_in.shape[1:], jnp.float32)
 
     for load in loads:
         load.wait()
@@ -110,14 +114,21 @@
 
     def prepare(t, _):
         here = pl.ds(pl.multiple_of(t * LANES, LANES), LANES)
-        wet = level_ids < wide(bot[pl.ds(t, 1), :])
+        bottom = wide(bot[pl.ds(t, 1), :])
+        turn = wide(cor[pl.ds(t, 1), :])
+        bot_of[t] = bottom
+        cor_of[t] = turn
+        wet = level_ids < bottom
         own[0, t] = jnp.where(wet, vel[0, :, here], 0.0)
         own[1, t] = jnp.where(wet, vel[1, :, here], 0.0)
         own[2, t] = den[:, here]
         eta[t] = jnp.where(lv == 0, wide(ele[pl.ds(t, 1), :], 8), 0.0)
         lane_pack = jnp.zeros((8, LANES), jnp.int32)
-        block_pack = jnp.zeros((8, LANES), jnp.int32)
-        packs = [jnp.zeros((8, LANES), jnp.float32) for _ in range(4)]
+        block_pack = bottom[:8]
+        packs = [jnp.zeros((8, LANES), jnp.float32) for _ in range(6)]
+        packs[2] = turn[:8]
+        flows = [[jnp.zeros((8, LANES), jnp.int32)] * 2 + [jnp.zeros((8, LANES), jnp.float32)] * 2
+                 for _ in range(flow_own.shape[1])]
         for k in range(near_count):
             slot = wide(near[k:k + 1, here])
             block = lax.shift_right_logical(slot, 7)
@@ -133,17 +144,52 @@
             mine = eight == k
             lane_pack = jnp.where(mine, lanes[:8], lane_pack)
             block_pack = jnp.where(mine, block[:8], block_pack)
-            packs = [jnp.where(mine, picked[i][:8], pack) for i, pack in zip((0, 1, 3, 4), packs)]
-        q_lanes[t] = lane_pack
-        q_block[t] = block_pack
-        for i in range(4):
-            q_weight[t, i] = packs[i]
+            packs = [jnp.where(mine, value[:8], pack) for value, pack in zip(picked, packs)]
+            flow = flows[k // 4]
+            first = 2 * (k % 4)
+            pair = jnp.logical_or(eight == first, eight == first + 1)
+            flow[0] = jnp.where(pair, lanes[:8], flow[0])
+            flow[1] = jnp.where(pair, block[:8], flow[1])
+            flow[2] = jnp.where(pair, jnp.where(odd, picked[1][:8], picked[0][:8]), flow[2])
+            flow[3] = jnp.where(pair, jnp.where(odd, picked[4][:8], picked[3][:8]), flow[3])
+        pack_lanes[t] = lane_pack
+        pack_block[t] = block_pack
+        for i in range(6):
+            pack_weight[t, i] = packs[i]
+        for j in range(flow_own.shape[1]):
+            flow_lanes[t, j], flow_block[t, j], flow_own[t, j], flow_halo[t, j] = flows[j]
         return 0
 
     lax.fori_loop(0, blocks, prepare, 0)
     wet_area = area[...] * jnp.where(bot[...] > 0, 1.0, 0.0)
+    area[...] = wet_area
     count = jnp.where(lv == 0, 1.0, 0.0)
     vol[...] = jnp.where(eight == STEPS, wide(jnp.sum(wet_area, axis=0, keepdims=True), 8) * count, 0.0)
+
+    def listed(side):
+        slot = wide(send[:, side * LANES:(side + 1) * LANES])
+        block = lax.shift_right_logical(slot, 7)
+        return jnp.bitwise_and(slot, LANES - 1), [block == b for b in range(1, blocks)]
+
+    def listed_tables():
+        for side in range(2):
+            t = blocks + side
+            lanes, masks = listed(side)
+            lanes, masks = lanes[:8], [mask[:8] for mask in masks]
+            found_lanes = pick([pack_lanes[b] for b in range(blocks)], lanes, masks)
+            found_block = pick([pack_block[b] for b in range(blocks)], lanes, masks)
+            found = [pick([pack_weight[b, i] for b in range(blocks)], lanes, masks) for i in range(6)]
+            pack_lanes[t] = found_lanes
+            pack_block[t] = found_block
+            for i in range(6):
+                pack_weight[t, i] = found[i]
+            bot_of[t] = wide(found_block[7:8])
+            cor_of[t] = wide(found[2][7:8])
+            for k in range(near_count):
+                lanes_of[t, k] = wide(found_lanes[k:k + 1])
+                block_of[t, k] = wide(found_block[k:k + 1])
+                for i in range(6):
+                    weight_of[t, k, i] = wide(found[i][k:k + 1])
 
     def version(q):
         return jnp.where(q > lv, 1, 0)
@@ -160,38 +206,43 @@
             send_sem=hs_send.at[s, side, q], recv_sem=hs_recv.at[s, 1 - side, slot],
             device_id={"space": ends[side], "level": q}, device_id_type=pl.DeviceIdType.MESH)
 
+    def adjoint_copy(side):
+        return pltpu.make_async_remote_copy(
+            src_ref=adjoint.at[side], dst_ref=adjoint_in.at[1 - side],
+            send_sem=adj_send.at[side], recv_sem=adj_recv.at[1 - side],
+            device_id={"space": ends[side], "level": lv}, device_id_type=pl.DeviceIdType.MESH)
+
     def peer_copy(s, q, slot):
         return pltpu.make_async_remote_copy(
             src_ref=peer_out.at[s, jnp.where(s < STEPS, version(q), 0)], dst_ref=peer.at[s, slot],
             send_sem=peer_send.at[s, q], recv_sem=peer_recv.at[s, slot],
             device_id={"space": sp, "level": q}, device_id_type=pl.DeviceIdType.MESH)
 
-    dev = sp * n_level + lv
-
-    def vol_copy(q, slot):
+    def vol_copy(d):
+        q = lax.rem(dev + d, n_dev)
         return pltpu.make_async_remote_copy(
-            src_ref=vol_line, dst_ref=vol_all.at[slot],
-            send_sem=vol_send.at[q], recv_sem=vol_recv.at[slot],
+            src_ref=vol_line, dst_ref=vol_all.at[d - 1], send_sem=vol_send, recv_sem=vol_recv,
             device_id={"space": q // n_level, "level": lax.rem(q, n_level)},
             device_id_type=pl.DeviceIdType.MESH)
 
-    def scalars(t, rho, level):
-        heavy = level + buoyancy * spread_sum(rho * thickness)
-        small[t] = jnp.where(odd, heavy, level)
-        return heavy
-
-    def stage_out(s):
-        for side in range(2):
-            slot = wide(send[:, side * LANES:(side + 1) * LANES])
-            lanes = jnp.bitwise_and(slot, LANES - 1)
-            block = lax.shift_right_logical(slot, 7)
-            masks = [block == b for b in range(1, blocks)]
-            for g in range(3):
-                out[s, side, g * rows:(g + 1) * rows] = pick([own[g, b] for b in range(blocks)], lanes, masks)
-            found = pick([small[b] for b in range(blocks)], lanes[:8], [m[:8] for m in masks])
-            out[s, side, 3 * rows:3 * rows + 8] = found
-            for i in range(2):
-                out_small[s, side, i] = found[i:i + 1]
+    def vol_every():
+        q = lax.rem(dev + 1, n_dev)
+        return pltpu.make_async_remote_copy(
+            src_ref=vol_all, dst_ref=vol_all, send_sem=vol_send, recv_sem=vol_recv,
+            device_id={"space": q // n_level, "level": lax.rem(q, n_level)},
+            device_id_type=pl.DeviceIdType.MESH)
+
+    def dense(rho, level):
+        return level + buoyancy * spread_sum(rho * thickness)
+
+    def stage(s, side, fields, level, heavy):
+        for g in range(3):
+            own[g, blocks + side] = fields[g]
+            out[s, side, g * rows:(g + 1) * rows] = fields[g]
+        eta[blocks + side] = level
+        out[s, side, 3 * rows:3 * rows + 8] = level
+        out_small[s, side, 0] = level[:1]
+        out_small[s, side, 1] = heavy[:1]
 
     def send_out(s):
         for side in range(2):
@@ -200,8 +251,6 @@
                 main_copy(s, side).start()
                 for q in others:
                     small_copy(s, side, q, lv).start()
-        for q in others:
-            peer_copy(s, q, lv).start()
 
     def close(s):
         for q in others:
@@ -212,6 +261,12 @@
                 main_copy(s, side).wait_send()
                 for q in others:
                     small_copy(s, side, q, lv).wait_send()
+
+    def gathered(sums, diff, weights):
+        east, north, smooth = weights
+        return [sums[0] + smooth * diff[0], sums[1] + smooth * diff[1], sums[2] + smooth * diff[2],
+                sums[3] + east * diff[2], sums[4] + north * diff[2],
+                sums[5] + (east * diff[0] + north * diff[1])]
 
     def own_parts():
         def body(t, _):
@@ -227,27 +282,23 @@
             for i in range(6):
                 part[t, i] = sums[i]
             return 0
-        lax.fori_loop(0, blocks, body, 0)
-
-    def gathered(sums, diff, weights):
-        east, north, smooth = weights
-        return [sums[0] + smooth * diff[0], sums[1] + smooth * diff[1], sums[2] + smooth * diff[2],
-                sums[3] + east * diff[2], sums[4] + north * diff[2],
-                sums[5] + (east * diff[0] + north * diff[1])]
+        lax.fori_loop(0, targets, body, 0)
 
     def own_surface(s):
         total = peer_out[s, 0]
         for q in others:
             total = total + peer[s, q]
         q_sum[...] = total
-        for t in range(blocks):
-            q_of[t] = wide(q_sum[t:t + 1, :], 8)
-        tiles = [q_of[b] for b in range(blocks)]
-        for t in range(blocks):
-            block = q_block[t]
-            diff = pick(tiles, q_lanes[t], [block == b for b in range(1, blocks)]) - tiles[t]
-            q_part[t, 0] = q_weight[t, 0] * diff
-            q_part[t, 1] = q_weight[t, 1] * diff
+        tiles = [wide(q_sum[t:t + 1, :], 8) for t in range(blocks)]
+        for side in range(2):
+            lanes, masks = listed(side)
+            tiles.append(pick(tiles[:blocks], lanes[:8], [mask[:8] for mask in masks]))
+        for t in range(targets):
+            q_of[t] = tiles[t]
+            block = pack_block[t]
+            diff = pick(tiles[:blocks], pack_lanes[t], [block == b for b in range(1, blocks)]) - tiles[t]
+            q_part[t, 0] = pack_weight[t, 0] * diff
+            q_part[t, 1] = pack_weight[t, 1] * diff
 
     def receive(s):
         for side in range(2):
@@ -260,48 +311,53 @@
             total = halo[s, side, 3 * rows:3 * rows + 1]
             for q in others:
                 total = total + halo_small[s, side, q]
-            q_of[blocks + side] = wide(total, 8)
+            q_edge[side] = wide(total, 8)
+
+    def advance(s, t):
+        edges = [[halo[s, side, g * rows:(g + 1) * rows] for side in range(2)] for g in range(3)]
+        here = [own[g, t] for g in range(3)]
+        sums = [part[t, i] for i in range(6)]
+        for k in range(near_count):
+            lanes = lanes_of[t, k]
+            upper = block_of[t, k] == blocks + 1
+            diff = [jnp.where(upper, lane_gather(edges[g][1], lanes), lane_gather(edges[g][0], lanes)) - here[g]
+                    for g in range(3)]
+            sums = gathered(sums, diff, [weight_of[t, k, 3 + i] for i in range(3)])
+        lap0, lap1, lap2, east2, north2, flow = sums
+        lanes = pack_lanes[t]
+        diff = jnp.where(pack_block[t] == blocks + 1, lane_gather(q_edge[1], lanes),
+                         lane_gather(q_edge[0], lanes)) - q_of[t]
+        slope0 = spread_sum(q_part[t, 0] + pack_weight[t, 3] * diff)
+        slope1 = spread_sum(q_part[t, 1] + pack_weight[t, 4] * diff)
+        bottom, turn = bot_of[t], cor_of[t]
+        drag = jnp.where(level_ids == bottom - 1, drag_rate, 0.0)
+        u, v, rho = here
+        east3, north3 = thickness * east2, thickness * north2
+        east3 = slope0 + buoyancy * (running_sum(east3, rows, row_ids) - 0.5 * east3)
+        north3 = slope1 + buoyancy * (running_sum(north3, rows, row_ids) - 0.5 * north3)
+        push0 = -east3 + turn * v + lap0 - drag * u
+        push1 = -north3 - turn * u + lap1 - drag * v
+        wet = level_ids < bottom
+        fields = (jnp.where(wet, u + time_step * push0, 0.0), jnp.where(wet, v + time_step * push1, 0.0),
+                  rho + time_step * (lap2 - u * east2 - v * north2))
+        diverge = spread_sum(thickness * flow)
+        level = eta[t] - time_step * jnp.where(bottom[:8] > 0, diverge, 0.0)
+        return fields, diverge, level, dense(fields[2], level)
+
+    def finish_listed(s):
+        for side in range(2):
+            fields, _, level, heavy = advance(s, blocks + side)
+            stage(s + 1, side, fields, level, heavy)
 
     def finish(s):
-        edges = [[halo[s, side, g * rows:(g + 1) * rows] for side in range(2)] for g in range(3)]
-        edges.append([q_of[blocks], q_of[blocks + 1]])
-
         def body(t, carry):
             volume, light, heavy = carry
-            here = [own[g, t] for g in range(3)]
-            sums = [part[t, i] for i in range(6)]
-            for k in range(near_count):
-                lanes = lanes_of[t, k]
-                upper = block_of[t, k] == blocks + 1
-                diff = [jnp.where(upper, lane_gather(edges[g][1], lanes), lane_gather(edges[g][0], lanes)) - here[g]
-                        for g in range(3)]
-                sums = gathered(sums, diff, [weight_of[t, k, 3 + i] for i in range(3)])
-            lap0, lap1, lap2, east2, north2, flow = sums
-            lanes = q_lanes[t]
-            diff = jnp.where(q_block[t] == blocks + 1, lane_gather(edges[3][1], lanes),
-                             lane_gather(edges[3][0], lanes)) - q_of[t]
-            slope0 = spread_sum(q_part[t, 0] + q_weight[t, 2] * diff)
-            slope1 = spread_sum(q_part[t, 1] + q_weight[t, 3] * diff)
-            bottom = wide(bot[pl.ds(t, 1), :])
-            turn = wide(cor[pl.ds(t, 1), :])
-            drag = jnp.where(level_ids == bottom - 1, drag_rate, 0.0)
-            u, v, rho = here
-            east3, north3 = thickness * east2, thickness * north2
-            east3 = slope0 + buoyancy * (running_sum(east3, rows, row_ids) - 0.5 * east3)
-            north3 = slope1 + buoyancy * (running_sum(north3, rows, row_ids) - 0.5 * north3)
-            push0 = -east3 + turn * v + lap0 - drag * u
-            push1 = -north3 - turn * u + lap1 - drag * v
-            wet = level_ids < bottom
-            own[0, t] = jnp.where(wet, u + time_step * push0, 0.0)
-            own[1, t] = jnp.where(wet, v + time_step * push1, 0.0)
-            fresh = rho + time_step * (lap2 - u * east2 - v * north2)
-            own[2, t] = fresh
-            diverge = jnp.where(bottom[:8] > 0, spread_sum(thickness * flow), 0.0)
-            level = eta[t] - time_step * diverge
+            fields, diverge, level, more = advance(s, t)
+            for g in range(3):
+                own[g, t] = fields[g]
             eta[t] = level
-            dense = scalars(t, fresh, level)
             return (volume + wide(area[pl.ds(t, 1), :], 8) * diverge,
-                    jnp.where(eight == t, level, light), jnp.where(eight == t, dense, heavy))
+                    jnp.where(eight == t, level, light), jnp.where(eight == t, more, heavy))
 
         zero = jnp.zeros((8, LANES), jnp.float32)
         volume, light, heavy = lax.fori_loop(0, blocks, body, (zero, zero, zero), unroll=True)
@@ -309,54 +365,118 @@
         peer_out[s + 1, 0] = light
         peer_out[s + 1, 1] = heavy
 
+    def make_adjoint():
+        ids = lax.broadcasted_iota(jnp.int32, (2 * LANES, LANES), 0) + blocks * LANES
+
+        def body(t, total):
+            weight = wide(area[pl.ds(t, 1), :], 8)
+            for k in range(near_count):
+                slot = block_of[t, k][:1] * LANES + lanes_of[t, k][:1]
+                hot = jnp.where(ids == jnp.broadcast_to(slot, ids.shape), 1.0, 0.0).astype(jnp.bfloat16)
+                value = jnp.where(odd, weight_of[t, k, 4][:8], weight_of[t, k, 3][:8]) * weight
+                high = value.astype(jnp.bfloat16).astype(jnp.float32)
+                value = value - high
+                middle = value.astype(jnp.bfloat16).astype(jnp.float32)
+                value = value - middle
+                value = jnp.where(eight < 2, high, jnp.where(eight < 4, middle, jnp.where(eight < 6, value, 0.0)))
+                total = total + lax.dot_general(
+                    value.astype(jnp.bfloat16), hot, (((1,), (1,)), ((), ())), preferred_element_type=jnp.float32)
+            return total
+
+        total = lax.fori_loop(0, blocks, body, jnp.zeros((8, 2 * LANES), jnp.float32))
+        total = total + pltpu.roll(total, 4, 0)
+        total = total + pltpu.roll(total, 2, 0)
+        for side in range(2):
+            adjoint[side] = total[:, side * LANES:(side + 1) * LANES]
+            @pl.when(has[side])
+            def _():
+                adjoint_copy(side).start()
+
+    def transport(t):
+        return jnp.where(odd, spread_sum(thickness * own[1, t])[:8], spread_sum(thickness * own[0, t])[:8])
+
+    def start_volume():
+        for side in range(2):
+            @pl.when(has[side])
+            def _():
+                adjoint_copy(1 - side).wait_recv()
+        tiles = [transport(t) for t in range(blocks)]
+        volume = jnp.zeros((8, LANES), jnp.float32)
+        for t in range(blocks):
+            total = jnp.zeros((8, LANES), jnp.float32)
+            for j in range(flow_own.shape[1]):
+                block = flow_block[t, j]
+                found = pick(tiles, flow_lanes[t, j], [block == b for b in range(1, blocks)])
+                total = total + (flow_own[t, j] * (found - tiles[t]) - flow_halo[t, j] * tiles[t])
+            volume = volume + wide(area[t:t + 1, :], 8) * total
+        for side in range(2):
+            volume = volume + jnp.where(eight < 2, adjoint_in[side] * transport(blocks + side), 0.0)
+        sums = jnp.sum(jnp.where(eight == STEPS - 1, spread_sum(volume), vol[...]), axis=1, keepdims=True)
+        line = jnp.zeros((1, LANES), jnp.float32)
+        for i in range(STEPS + 1):
+            line = jnp.where(lane_ids == i, sums[i:i + 1], line)
+        vol_line[...] = line
+        pl.semaphore_wait(column_in, len(row))
+
+        def start(d, _):
+            vol_copy(d).start()
+            return 0
+
+        lax.fori_loop(1, n_dev, start, 0)
+
     def first(t, carry):
         light, heavy = carry
-        dense = scalars(t, own[2, t], eta[t])
-        return jnp.where(eight == t, eta[t], light), jnp.where(eight == t, dense, heavy)
+        more = dense(own[2, t], eta[t])
+        small[t] = jnp.where(odd, more, eta[t])
+        return jnp.where(eight == t, eta[t], light), jnp.where(eight == t, more, heavy)
 
     zero = jnp.zeros((8, LANES), jnp.float32)
     light, heavy = lax.fori_loop(0, blocks, first, (zero, zero), unroll=True)
     peer_out[0, 0] = light
     peer_out[0, 1] = heavy
-    stage_out(0)
+    for side in range(2):
+        lanes, masks = listed(side)
+        fields = [pick([own[g, b] for b in range(blocks)], lanes, masks) for g in range(3)]
+        found = pick([small[b] for b in range(blocks)], lanes[:8], [m[:8] for m in masks])
+        stage(0, side, fields, wide(found[:1], 8), wide(found[1:2], 8))
 
     expected = len(row) + len(column) + n_level * (low + high)
     pl.semaphore_wait(barrier, expected)
+    send_out(0)
+    for q in others:
+        peer_copy(0, q, lv).start()
     for q, level in row:
         pl.semaphore_signal(column_in, inc=1, device_id={"space": q, "level": level})
+    listed_tables()
 
     def step(s, _):
-        send_out(s)
+        @pl.when(s == STEPS - 1)
+        def _():
+            start_volume()
+
         own_parts()
+
+        @pl.when(s == 0)
+        def _():
+            make_adjoint()
+
         for q in others:
             peer_copy(s, q, q).wait_recv()
         own_surface(s)
         receive(s)
-        finish(s)
 
         @pl.when(s < STEPS - 1)
         def _():
-            stage_out(s + 1)
-
+            finish_listed(s)
+            send_out(s + 1)
+
+        finish(s)
+        for q in others:
+            peer_copy(s + 1, q, lv).start()
         close(s)
         return 0
 
     lax.fori_loop(0, STEPS, step, 0)
-
-    sums = jnp.sum(vol[...], axis=1, keepdims=True)
-    line = jnp.zeros((1, LANES), jnp.float32)
-    for i in range(STEPS + 1):
-        line = jnp.where(lane_ids == i, sums[i:i + 1], line)
-    vol_line[...] = line
-    pl.semaphore_wait(column_in, len(row))
-    for q in others:
-        peer_copy(STEPS, q, lv).start()
-
-    def start(d, _):
-        vol_copy(lax.rem(dev + d, n_dev), dev).start()
-        return 0
-
-    lax.fori_loop(1, n_dev, start, 0)
 
     for t in range(blocks):
         here = slice(t * LANES, (t + 1) * LANES)
@@ -368,25 +488,20 @@
     for q in others:
         peer_copy(STEPS, q, q).wait_recv()
         level = level + peer[STEPS, q]
-
-    def collect(d, total):
-        q = lax.rem(dev + d, n_dev)
-        vol_copy(q, q).wait_recv()
-        return total + vol_all[q]
-
-    total = lax.fori_loop(1, n_dev, collect, vol_line[...])
+    for q in others:
+        peer_copy(STEPS, q, lv).wait_send()
+    for side in range(2):
+        @pl.when(has[side])
+        def _():
+            adjoint_copy(side).wait_send()
+
+    vol_every().wait_send()
+    vol_every().wait_recv()
+    total = lax.fori_loop(0, n_dev - 1, lambda d, total: total + vol_all[d], vol_line[...], unroll=n_dev <= 64)
     drifts = total / total[:, STEPS:STEPS + 1]
     shift = jnp.sum(jnp.where(lane_ids < STEPS, drifts, 0.0), axis=1, keepdims=True)
     ele_out[...] = level + time_step * shift
     drift_out[...] = drifts
-    for q in others:
-        peer_copy(STEPS, q, lv).wait_send()
-
-    def done(d, _):
-        vol_copy(lax.rem(dev + d, n_dev), dev).wait_send()
-        return 0
-
-    lax.fori_loop(1, n_dev, done, 0)
 
 
 def emit(vel, den, ele, drift, vel_out, den_out, ele_out, drift_out):
@@ -406,6 +521,8 @@
         rows, nodes = density.shape
         blocks = nodes // LANES
         near_count = neighbours.shape[0]
+        assert near_count < 8 and rows == 8
+        packs = -(-near_count // 4)
         f32, i32 = jnp.float32, jnp.int32
         plane = (blocks, LANES)
         vmem = pl.BlockSpec(memory_space=pltpu.VMEM)
@@ -428,17 +545,24 @@
             in_specs=[hbm] * 11,
             out_specs=(vmem, vmem, vmem, vmem),
             scratch_shapes=[
-                pltpu.VMEM((3, blocks) + tile, f32),
-                pltpu.VMEM((blocks,) + pack, f32),
-                pltpu.VMEM((blocks, near_count) + tile, i32),
-                pltpu.VMEM((blocks, near_count) + tile, i32),
-                pltpu.VMEM((blocks, near_count, 6) + tile, f32),
-                pltpu.VMEM((blocks,) + pack, i32),
-                pltpu.VMEM((blocks,) + pack, i32),
-                pltpu.VMEM((blocks, 4) + pack, f32),
-                pltpu.VMEM((blocks, 6) + tile, f32),
-                pltpu.VMEM((blocks, 2) + pack, f32),
+                pltpu.VMEM((3, blocks + 2) + tile, f32),
                 pltpu.VMEM((blocks + 2,) + pack, f32),
+                pltpu.VMEM((blocks + 2,) + tile, f32),
+                pltpu.VMEM((blocks + 2,) + tile, i32),
+                pltpu.VMEM((blocks + 2, near_count) + tile, i32),
+                pltpu.VMEM((blocks + 2, near_count) + tile, i32),
+                pltpu.VMEM((blocks + 2, near_count, 6) + tile, f32),
+                pltpu.VMEM((blocks + 2,) + pack, i32),
+                pltpu.VMEM((blocks + 2,) + pack, i32),
+                pltpu.VMEM((blocks + 2, 6) + pack, f32),
+                pltpu.VMEM((blocks, packs) + pack, i32),
+                pltpu.VMEM((blocks, packs) + pack, i32),
+                pltpu.VMEM((blocks, packs) + pack, f32),
+                pltpu.VMEM((blocks, packs) + pack, f32),
+                pltpu.VMEM((blocks + 2, 6) + tile, f32),
+                pltpu.VMEM((blocks + 2, 2) + pack, f32),
+                pltpu.VMEM((blocks + 2,) + pack, f32),
+                pltpu.VMEM((2,) + pack, f32),
                 pltpu.VMEM(plane, f32),
                 pltpu.VMEM((blocks,) + pack, f32),
                 pltpu.VMEM((STEPS, 2, 3 * rows + 8, LANES), f32),
@@ -449,11 +573,14 @@
                 pltpu.VMEM((STEPS + 1, n_level) + plane, f32),
                 pltpu.VMEM(pack, f32),
                 pltpu.VMEM((1, LANES), f32),
-                pltpu.VMEM((n_dev, 1, LANES), f32),
+                pltpu.VMEM((n_dev - 1, 1, LANES), f32),
+                pltpu.VMEM((2,) + pack, f32),
+                pltpu.VMEM((2,) + pack, f32),
                 dma((STEPS, 2)), dma((STEPS, 2)),
                 dma((STEPS, 2, n_level)), dma((STEPS, 2, n_level)),
                 dma((STEPS + 1, n_level)), dma((STEPS + 1, n_level)),
-                dma((n_dev,)), dma((n_dev,)),
+                dma, dma,
+                dma((2,)), dma((2,)),
                 pltpu.SemaphoreType.REGULAR,
                 dma((11,)),
                 pltpu.SMEM(thickness.shape, f32),

time: 30.5 us -> 25.6 us (0.84)
  Pallas kernels: 29.7 us -> 24.8 us
    pallas_call x1, Pallas kernels: 29.1 us -> 24.2 us  [local(): pl.pallas_call(functools.partial(kernel, n_space, n_level, width, rows, b...]
where the time goes in v1:
time: 25.6 us; the launch traced here: 25.5 us
  Pallas kernels  24.8 us (97%)
  between operations  0.64 us (2%)
    pallas_call x1, Pallas kernels, local(): pl.pallas_call(functools.partial(kernel, n_space, n_level, width, rows, b...  24.2 us
    pallas_call x1, Pallas kernels, local(): pl.pallas_call(emit, out_shape=(jax.ShapeDtypeStruct(velocity.shape, f32)...  0.65 us

profile of v1, /device:TPU:0, one launch (start us, length us, event | category | flops | bytes accessed | tf_op | source)
XLA Modules:
  0.0 25.5 jit_solution(14191732680687430221)
XLA Ops:
  0.6 24.2 %shard_map.138 = (f32[2,8,1024]{2,1,0:T(8,128)S(1)}, f32[8,1024]{1,0:T(8,128)S(1)}, f32[8,128]{1,0:T(8,128)S(1)}, f32[1,128]{1,0:T(1,128)S(1)}) custom-call(f32[2,8,1024]{2,1,0:T(8,128)} %vel.1, f32[8,1024]{1,0:T(8,128)} %den.1, f32[8,128]{1,0:T(8,128)} %bitcast.8, f32[6,2,1024]{2,1,0:T(2,128)} %bitcast.7, f32[6,1024]{1,0:T(8,128)} %lap.1, ...), custom_call_target="tpu_custom_call" | custom-call | tf_op jit(solution)/shard_map/pallas_call | solution.py:537
  24.8 0.6 %shard_map.139 = (f32[2,8,1024]{2,1,0:T(8,128)}, f32[8,1024]{1,0:T(8,128)}, f32[8,128]{1,0:T(8,128)}, f32[1,4]{1,0:T(1,128)}) custom-call(f32[2,8,1024]{2,1,0:T(8,128)S(1)} %get-tuple-element.12.vel, f32[8,1024]{1,0:T(8,128)S(1)} %get-tuple-element.13.den, f32[8,128]{1,0:T(8,128)S(1)} %get-tuple-element.14.ele, f32[1,128]{1,0:T(1,128)S(1)} %get-tuple-element.15.drift), custom_call_target="tpu_custom_call" | custom-call | tf_op jit(solution)/shard_map/pallas_call | solution.py:591

commit v2 on v1

--- a/solution.py
+++ b/solution.py
@@ -50,7 +50,7 @@
     own, eta, cor_of, bot_of, lanes_of, block_of, weight_of, pack_lanes, pack_block, pack_weight,
     flow_lanes, flow_block, flow_own, flow_halo,
     part, q_part, q_of, q_edge, q_sum, small, out, out_small, halo, halo_small, peer_out, peer,
-    vol, vol_line, vol_all, adjoint, adjoint_in,
+    vol, vol_line, vol_all, adjoint_sum, adjoint, adjoint_in,
     main_send, main_recv, hs_send, hs_recv, peer_send, peer_recv, vol_send, vol_recv, adj_send, adj_recv, column_in,
     load_sem, thick_in, *loaded,
 ):
@@ -104,8 +104,9 @@
             halo_small[:, side] = jnp.zeros(halo_small.shape[:1] + halo_small.shape[2:], jnp.float32)
             adjoint_in[side] = jnp.zeros(adjoint_in.shape[1:], jnp.float32)
 
-    for load in loads:
-        load.wait()
+    early = (0, 1, 2, 7, 8, 10)
+    for i in early:
+        loads[i].wait()
     vel, den, ele, grad, lap, cor, area, send, near, bot = loaded
 
     thickness = jnp.zeros((rows, LANES), jnp.float32)
@@ -114,15 +115,9 @@
 
     def prepare(t, _):
         here = pl.ds(pl.multiple_of(t * LANES, LANES), LANES)
-        bottom = wide(bot[pl.ds(t, 1), :])
+        bottom = bot_of[t]
         turn = wide(cor[pl.ds(t, 1), :])
-        bot_of[t] = bottom
         cor_of[t] = turn
-        wet = level_ids < bottom
-        own[0, t] = jnp.where(wet, vel[0, :, here], 0.0)
-        own[1, t] = jnp.where(wet, vel[1, :, here], 0.0)
-        own[2, t] = den[:, here]
-        eta[t] = jnp.where(lv == 0, wide(ele[pl.ds(t, 1), :], 8), 0.0)
         lane_pack = jnp.zeros((8, LANES), jnp.int32)
         block_pack = bottom[:8]
         packs = [jnp.zeros((8, LANES), jnp.float32) for _ in range(6)]
@@ -160,11 +155,6 @@
             flow_lanes[t, j], flow_block[t, j], flow_own[t, j], flow_halo[t, j] = flows[j]
         return 0
 
-    lax.fori_loop(0, blocks, prepare, 0)
-    wet_area = area[...] * jnp.where(bot[...] > 0, 1.0, 0.0)
-    area[...] = wet_area
-    count = jnp.where(lv == 0, 1.0, 0.0)
-    vol[...] = jnp.where(eight == STEPS, wide(jnp.sum(wet_area, axis=0, keepdims=True), 8) * count, 0.0)
 
     def listed(side):
         slot = wide(send[:, side * LANES:(side + 1) * LANES])
@@ -197,13 +187,13 @@
     def main_copy(s, side):
         return pltpu.make_async_remote_copy(
             src_ref=out.at[s, side], dst_ref=halo.at[s, 1 - side],
-            send_sem=main_send.at[s, side], recv_sem=main_recv.at[s, 1 - side],
+            send_sem=main_send.at[side], recv_sem=main_recv.at[lax.rem(s, 2), 1 - side],
             device_id={"space": ends[side], "level": lv}, device_id_type=pl.DeviceIdType.MESH)
 
     def small_copy(s, side, q, slot):
         return pltpu.make_async_remote_copy(
             src_ref=out_small.at[s, side, version(q)], dst_ref=halo_small.at[s, 1 - side, slot],
-            send_sem=hs_send.at[s, side, q], recv_sem=hs_recv.at[s, 1 - side, slot],
+            send_sem=hs_send.at[side, q], recv_sem=hs_recv.at[lax.rem(s, 2), 1 - side, slot],
             device_id={"space": ends[side], "level": q}, device_id_type=pl.DeviceIdType.MESH)
 
     def adjoint_copy(side):
@@ -215,11 +205,18 @@
     def peer_copy(s, q, slot):
         return pltpu.make_async_remote_copy(
             src_ref=peer_out.at[s, jnp.where(s < STEPS, version(q), 0)], dst_ref=peer.at[s, slot],
-            send_sem=peer_send.at[s, q], recv_sem=peer_recv.at[s, slot],
+            send_sem=peer_send.at[q], recv_sem=peer_recv.at[lax.rem(s, 2), slot],
             device_id={"space": sp, "level": q}, device_id_type=pl.DeviceIdType.MESH)
 
+    bits = n_dev.bit_length() - 1
+    mirror = n_dev == 1 << bits and n_dev <= 64
+    flips = [(1 - 2 * lax.rem(dev // (1 << i), 2)) * (1 << i) for i in range(bits)] if mirror else []
+
     def vol_copy(d):
-        q = lax.rem(dev + d, n_dev)
+        if mirror:
+            q = dev + sum(flips[i] for i in range(bits) if d >> i & 1)
+        else:
+            q = lax.rem(dev + d, n_dev)
         return pltpu.make_async_remote_copy(
             src_ref=vol_line, dst_ref=vol_all.at[d - 1], send_sem=vol_send, recv_sem=vol_recv,
             device_id={"space": q // n_level, "level": lax.rem(q, n_level)},
@@ -282,7 +279,13 @@
             for i in range(6):
                 part[t, i] = sums[i]
             return 0
-        lax.fori_loop(0, targets, body, 0)
+        several = max(d for d in (1, 2, 5) if targets % d == 0)
+
+        def bodies(i, _):
+            for j in range(several):
+                body(i * several + j, 0)
+            return 0
+        lax.fori_loop(0, targets // several, bodies, 0)
 
     def own_surface(s):
         total = peer_out[s, 0]
@@ -365,7 +368,7 @@
         peer_out[s + 1, 0] = light
         peer_out[s + 1, 1] = heavy
 
-    def make_adjoint():
+    def make_adjoint(s):
         ids = lax.broadcasted_iota(jnp.int32, (2 * LANES, LANES), 0) + blocks * LANES
 
         def body(t, total):
@@ -383,12 +386,14 @@
                     value.astype(jnp.bfloat16), hot, (((1,), (1,)), ((), ())), preferred_element_type=jnp.float32)
             return total
 
-        total = lax.fori_loop(0, blocks, body, jnp.zeros((8, 2 * LANES), jnp.float32))
+        half = -(-blocks // 2)
+        total = lax.fori_loop(s * half, jnp.minimum((s + 1) * half, blocks), body, adjoint_sum[...])
+        adjoint_sum[...] = total
         total = total + pltpu.roll(total, 4, 0)
         total = total + pltpu.roll(total, 2, 0)
         for side in range(2):
             adjoint[side] = total[:, side * LANES:(side + 1) * LANES]
-            @pl.when(has[side])
+            @pl.when(jnp.logical_and(has[side], s == 1))
             def _():
                 adjoint_copy(side).start()
 
@@ -418,20 +423,35 @@
         vol_line[...] = line
         pl.semaphore_wait(column_in, len(row))
 
-        def start(d, _):
-            vol_copy(d).start()
-            return 0
-
-        lax.fori_loop(1, n_dev, start, 0)
+        if mirror:
+            for d in range(n_dev - 1, 0, -1):
+                vol_copy(d).start()
+        else:
+            def start(d, _):
+                vol_copy(d).start()
+                return 0
+
+            lax.fori_loop(1, n_dev, start, 0)
 
     def first(t, carry):
         light, heavy = carry
-        more = dense(own[2, t], eta[t])
-        small[t] = jnp.where(odd, more, eta[t])
-        return jnp.where(eight == t, eta[t], light), jnp.where(eight == t, more, heavy)
+        here = slice(t * LANES, (t + 1) * LANES)
+        bottom = wide(bot[t:t + 1, :])
+        bot_of[t] = bottom
+        wet = level_ids < bottom
+        own[0, t] = jnp.where(wet, vel[0, :, here], 0.0)
+        own[1, t] = jnp.where(wet, vel[1, :, here], 0.0)
+        own[2, t] = den[:, here]
+        level = jnp.where(lv == 0, wide(ele[t:t + 1, :], 8), 0.0)
+        eta[t] = level
+        more = dense(own[2, t], level)
+        small[t] = jnp.where(odd, more, level)
+        return jnp.where(eight == t, level, light), jnp.where(eight == t, more, heavy)
 
     zero = jnp.zeros((8, LANES), jnp.float32)
-    light, heavy = lax.fori_loop(0, blocks, first, (zero, zero), unroll=True)
+    light, heavy = zero, zero
+    for t in range(blocks):
+        light, heavy = first(t, (light, heavy))
     peer_out[0, 0] = light
     peer_out[0, 1] = heavy
     for side in range(2):
@@ -447,6 +467,15 @@
         peer_copy(0, q, lv).start()
     for q, level in row:
         pl.semaphore_signal(column_in, inc=1, device_id={"space": q, "level": level})
+    for i in range(len(loads)):
+        if i not in early:
+            loads[i].wait()
+    lax.fori_loop(0, blocks, prepare, 0)
+    wet_area = area[...] * jnp.where(bot[...] > 0, 1.0, 0.0)
+    area[...] = wet_area
+    count = jnp.where(lv == 0, 1.0, 0.0)
+    vol[...] = jnp.where(eight == STEPS, wide(jnp.sum(wet_area, axis=0, keepdims=True), 8) * count, 0.0)
+    adjoint_sum[...] = jnp.zeros((8, 2 * LANES), jnp.float32)
     listed_tables()
 
     def step(s, _):
@@ -456,15 +485,17 @@
 
         own_parts()
 
-        @pl.when(s == 0)
+        @pl.when(s < 2)
         def _():
-            make_adjoint()
+            make_adjoint(s)
 
         for q in others:
             peer_copy(s, q, q).wait_recv()
         own_surface(s)
         receive(s)
 
+        close(s)
+
         @pl.when(s < STEPS - 1)
         def _():
             finish_listed(s)
@@ -473,7 +504,6 @@
         finish(s)
         for q in others:
             peer_copy(s + 1, q, lv).start()
-        close(s)
         return 0
 
     lax.fori_loop(0, STEPS, step, 0)
@@ -574,11 +604,12 @@
                 pltpu.VMEM(pack, f32),
                 pltpu.VMEM((1, LANES), f32),
                 pltpu.VMEM((n_dev - 1, 1, LANES), f32),
+                pltpu.VMEM((8, 2 * LANES), f32),
                 pltpu.VMEM((2,) + pack, f32),
                 pltpu.VMEM((2,) + pack, f32),
-                dma((STEPS, 2)), dma((STEPS, 2)),
-                dma((STEPS, 2, n_level)), dma((STEPS, 2, n_level)),
-                dma((STEPS + 1, n_level)), dma((STEPS + 1, n_level)),
+                dma((2,)), dma((2, 2)),
+                dma((2, n_level)), dma((2, 2, n_level)),
+                dma((n_level,)), dma((2, n_level)),
                 dma, dma,
                 dma((2,)), dma((2,)),
                 pltpu.SemaphoreType.REGULAR,

time: 25.6 us -> 24.2 us (0.945)
  Pallas kernels: 24.8 us -> 23.4 us
    pallas_call x1, Pallas kernels: 24.2 us -> 22.8 us  [local(): pl.pallas_call(functools.partial(kernel, n_space, n_level, width, rows, b...]
where the time goes in v2:
time: 24.2 us; the launch traced here: 24.1 us
  Pallas kernels  23.4 us (97%)
  between operations  0.64 us (3%)
    pallas_call x1, Pallas kernels, local(): pl.pallas_call(functools.partial(kernel, n_space, n_level, width, rows, b...  22.8 us
    pallas_call x1, Pallas kernels, local(): pl.pallas_call(emit, out_shape=(jax.ShapeDtypeStruct(velocity.shape, f32)...  0.65 us

profile of v2, /device:TPU:0, one launch (start us, length us, event | category | flops | bytes accessed | tf_op | source)
XLA Modules:
  0.0 24.1 jit_solution(7160504398152084413)
XLA Ops:
  0.6 22.8 %shard_map.138 = (f32[2,8,1024]{2,1,0:T(8,128)S(1)}, f32[8,1024]{1,0:T(8,128)S(1)}, f32[8,128]{1,0:T(8,128)S(1)}, f32[1,128]{1,0:T(1,128)S(1)}) custom-call(f32[2,8,1024]{2,1,0:T(8,128)} %vel.1, f32[8,1024]{1,0:T(8,128)} %den.1, f32[8,128]{1,0:T(8,128)} %bitcast.8, f32[6,2,1024]{2,1,0:T(2,128)} %bitcast.7, f32[6,1024]{1,0:T(8,128)} %lap.1, ...), custom_call_target="tpu_custom_call" | custom-call | tf_op jit(solution)/shard_map/pallas_call | solution.py:567
  23.4 0.6 %shard_map.139 = (f32[2,8,1024]{2,1,0:T(8,128)}, f32[8,1024]{1,0:T(8,128)}, f32[8,128]{1,0:T(8,128)}, f32[1,4]{1,0:T(1,128)}) custom-call(f32[2,8,1024]{2,1,0:T(8,128)S(1)} %get-tuple-element.12.vel, f32[8,1024]{1,0:T(8,128)S(1)} %get-tuple-element.13.den, f32[8,128]{1,0:T(8,128)S(1)} %get-tuple-element.14.ele, f32[1,128]{1,0:T(1,128)S(1)} %get-tuple-element.15.drift), custom_call_target="tpu_custom_call" | custom-call | tf_op jit(solution)/shard_map/pallas_call | solution.py:622

commit v3 on v2

--- a/solution.py
+++ b/solution.py
@@ -44,14 +44,14 @@
 
 
 def kernel(
-    n_space, n_level, width, rows, blocks, near_count,
+    n_space, n_level, rows, blocks, near_count,
     vel, den, ele, grad, lap, cor, area, thick, send, near, bot,
     vel_out, den_out, ele_out, drift_out,
     own, eta, cor_of, bot_of, lanes_of, block_of, weight_of, pack_lanes, pack_block, pack_weight,
     flow_lanes, flow_block, flow_own, flow_halo,
     part, q_part, q_of, q_edge, q_sum, small, out, out_small, halo, halo_small, peer_out, peer,
-    vol, vol_line, vol_all, adjoint_sum, adjoint, adjoint_in,
-    main_send, main_recv, hs_send, hs_recv, peer_send, peer_recv, vol_send, vol_recv, adj_send, adj_recv, column_in,
+    flow, vol, vol_line, line, lines, adjoint_sum, adjoint, adjoint_in,
+    main_send, main_recv, hs_send, hs_recv, peer_send, peer_recv, line_send, line_recv, adj_send, adj_recv, ready,
     load_sem, thick_in, *loaded,
 ):
     sp = lax.axis_index("space")
@@ -67,17 +67,27 @@
 
     barrier = pltpu.get_barrier_semaphore()
 
-    mine, place = sp // width, lax.rem(sp, width)
-    column = [(lax.rem(sp + d * width, n_space), lv) for d in range(1, n_space // width)]
-    row = [(mine * width + lax.rem(place + d, width), lax.rem(lv + e, n_level))
-           for d in range(width) for e in range(n_level) if d or e]
-    for q, level in row + column:
-        pl.semaphore_signal(barrier, inc=1, device_id={"space": q, "level": level})
     for side in range(2):
         @pl.when(has[side])
         def _():
             for q in [lv] + others:
                 pl.semaphore_signal(barrier, inc=1, device_id={"space": ends[side], "level": q})
+    for q in others:
+        pl.semaphore_signal(barrier, inc=1, device_id={"space": sp, "level": q})
+
+    rounds = (n_space - 1).bit_length()
+
+    def reached(j):
+        return [(sp - (1 << j), sp >= 1 << j), (sp + (1 << j), sp + (1 << j) < n_space)]
+
+    def tell(j):
+        for q, there in reached(j):
+            @pl.when(there)
+            def _():
+                pl.semaphore_signal(ready.at[j], inc=1, device_id={"space": q, "level": lv})
+
+    def hear(j):
+        pl.semaphore_wait(ready.at[j], sum(jnp.where(there, 1, 0) for _, there in reached(j)))
 
     loads = [
         pltpu.make_async_copy(ref, buffer, load_sem.at[i])
@@ -209,25 +219,49 @@
             device_id={"space": sp, "level": q}, device_id_type=pl.DeviceIdType.MESH)
 
     bits = n_dev.bit_length() - 1
-    mirror = n_dev == 1 << bits and n_dev <= 64
-    flips = [(1 - 2 * lax.rem(dev // (1 << i), 2)) * (1 << i) for i in range(bits)] if mirror else []
-
-    def vol_copy(d):
+    mirror = n_dev == 1 << bits and n_level == 1 << (n_level.bit_length() - 1) and n_dev <= 64
+    low_bits = n_level.bit_length() - 1
+    flips = ([(1 - 2 * lax.rem(lv // (1 << i), 2)) * (1 << i) for i in range(low_bits)]
+             + [(1 - 2 * lax.rem(sp // (1 << i), 2)) * (1 << i) for i in range(bits - low_bits)]) if mirror else []
+
+    def partner(d):
+        if not mirror:
+            q = lax.rem(dev + d, n_dev)
+            return {"space": q // n_level, "level": lax.rem(q, n_level)}
+        if not isinstance(d, int):
+            return {"space": 0, "level": 0}
+        low = low_bits
+        flip = [sum((flips[i] for i in bit if d >> i & 1), 0) for bit in (range(low), range(low, bits))]
+        return {"space": sp + flip[1], "level": lv + flip[0]}
+
+    def line_copy(d):
+        return pltpu.make_async_remote_copy(
+            src_ref=line, dst_ref=lines.at[d - 1], send_sem=line_send, recv_sem=line_recv,
+            device_id=partner(d), device_id_type=pl.DeviceIdType.MESH)
+
+    def send_lines():
         if mirror:
-            q = dev + sum(flips[i] for i in range(bits) if d >> i & 1)
+            for d in range(n_dev - 1, 0, -1):
+                line_copy(d).start()
         else:
-            q = lax.rem(dev + d, n_dev)
+            def start(d, _):
+                line_copy(d).start()
+                return 0
+
+            lax.fori_loop(1, n_dev, start, 0)
+
+    def every_line():
         return pltpu.make_async_remote_copy(
-            src_ref=vol_line, dst_ref=vol_all.at[d - 1], send_sem=vol_send, recv_sem=vol_recv,
-            device_id={"space": q // n_level, "level": lax.rem(q, n_level)},
-            device_id_type=pl.DeviceIdType.MESH)
-
-    def vol_every():
-        q = lax.rem(dev + 1, n_dev)
-        return pltpu.make_async_remote_copy(
-            src_ref=vol_all, dst_ref=vol_all, send_sem=vol_send, recv_sem=vol_recv,
-            device_id={"space": q // n_level, "level": lax.rem(q, n_level)},
-            device_id_type=pl.DeviceIdType.MESH)
+            src_ref=lines, dst_ref=lines, send_sem=line_send, recv_sem=line_recv,
+            device_id=partner(1), device_id_type=pl.DeviceIdType.MESH)
+
+    def add_lines():
+        if not mirror:
+            return lax.fori_loop(0, n_dev - 1, lambda d, total: total + lines[d], line[...])
+        terms = [line[...]] + [lines[d] for d in range(n_dev - 1)]
+        while len(terms) > 1:
+            terms = [sum(terms[i + 1:i + 2], terms[i]) for i in range(0, len(terms), 2)]
+        return terms[0]
 
     def dense(rho, level):
         return level + buoyancy * spread_sum(rho * thickness)
@@ -347,6 +381,9 @@
         level = eta[t] - time_step * jnp.where(bottom[:8] > 0, diverge, 0.0)
         return fields, diverge, level, dense(fields[2], level)
 
+    def transport(fields):
+        return jnp.where(odd, spread_sum(thickness * fields[1]), spread_sum(thickness * fields[0]))
+
     def finish_listed(s):
         for side in range(2):
             fields, _, level, heavy = advance(s, blocks + side)
@@ -358,6 +395,7 @@
             fields, diverge, level, more = advance(s, t)
             for g in range(3):
                 own[g, t] = fields[g]
+            flow[t] = transport(fields)
             eta[t] = level
             return (volume + wide(area[pl.ds(t, 1), :], 8) * diverge,
                     jnp.where(eight == t, level, light), jnp.where(eight == t, more, heavy))
@@ -369,13 +407,14 @@
         peer_out[s + 1, 1] = heavy
 
     def make_adjoint(s):
-        ids = lax.broadcasted_iota(jnp.int32, (2 * LANES, LANES), 0) + blocks * LANES
+        ids = lax.broadcasted_iota(jnp.int32, (2 * LANES, LANES), 0).astype(jnp.bfloat16)
 
         def body(t, total):
             weight = wide(area[pl.ds(t, 1), :], 8)
             for k in range(near_count):
-                slot = block_of[t, k][:1] * LANES + lanes_of[t, k][:1]
-                hot = jnp.where(ids == jnp.broadcast_to(slot, ids.shape), 1.0, 0.0).astype(jnp.bfloat16)
+                slot = jnp.maximum((block_of[t, k][:1] - blocks) * LANES + lanes_of[t, k][:1], -1)
+                slot = jnp.broadcast_to(slot.astype(jnp.bfloat16), ids.shape)
+                hot = jnp.where(ids == slot, jnp.bfloat16(1), jnp.bfloat16(0))
                 value = jnp.where(odd, weight_of[t, k, 4][:8], weight_of[t, k, 3][:8]) * weight
                 high = value.astype(jnp.bfloat16).astype(jnp.float32)
                 value = value - high
@@ -397,15 +436,19 @@
             def _():
                 adjoint_copy(side).start()
 
-    def transport(t):
-        return jnp.where(odd, spread_sum(thickness * own[1, t])[:8], spread_sum(thickness * own[0, t])[:8])
-
-    def start_volume():
+    def add_early():
+        sums = jnp.sum(vol[...], axis=1, keepdims=True)
+        total = jnp.zeros((1, LANES), jnp.float32)
+        for i in (*range(STEPS - 2), STEPS):
+            total = jnp.where(lane_ids == i, sums[i:i + 1], total)
+        vol_line[...] = total
+
+    def start_late():
         for side in range(2):
             @pl.when(has[side])
             def _():
                 adjoint_copy(1 - side).wait_recv()
-        tiles = [transport(t) for t in range(blocks)]
+        tiles = [flow[t] for t in range(blocks)]
         volume = jnp.zeros((8, LANES), jnp.float32)
         for t in range(blocks):
             total = jnp.zeros((8, LANES), jnp.float32)
@@ -415,23 +458,13 @@
                 total = total + (flow_own[t, j] * (found - tiles[t]) - flow_halo[t, j] * tiles[t])
             volume = volume + wide(area[t:t + 1, :], 8) * total
         for side in range(2):
-            volume = volume + jnp.where(eight < 2, adjoint_in[side] * transport(blocks + side), 0.0)
-        sums = jnp.sum(jnp.where(eight == STEPS - 1, spread_sum(volume), vol[...]), axis=1, keepdims=True)
-        line = jnp.zeros((1, LANES), jnp.float32)
-        for i in range(STEPS + 1):
-            line = jnp.where(lane_ids == i, sums[i:i + 1], line)
-        vol_line[...] = line
-        pl.semaphore_wait(column_in, len(row))
-
-        if mirror:
-            for d in range(n_dev - 1, 0, -1):
-                vol_copy(d).start()
-        else:
-            def start(d, _):
-                vol_copy(d).start()
-                return 0
-
-            lax.fori_loop(1, n_dev, start, 0)
+            lanes, masks = listed(side)
+            found = pick(tiles, lanes[:8], [mask[:8] for mask in masks])
+            volume = volume + jnp.where(eight < 2, adjoint_in[side] * found, 0.0)
+        volume = jnp.where(eight == 1, vol[...][STEPS - 2:STEPS - 1], spread_sum(volume))
+        line[...] = jnp.where(eight == 0, vol_line[...], volume)[:3]
+        hear(rounds - 1)
+        send_lines()
 
     def first(t, carry):
         light, heavy = carry
@@ -460,13 +493,11 @@
         found = pick([small[b] for b in range(blocks)], lanes[:8], [m[:8] for m in masks])
         stage(0, side, fields, wide(found[:1], 8), wide(found[1:2], 8))
 
-    expected = len(row) + len(column) + n_level * (low + high)
-    pl.semaphore_wait(barrier, expected)
+    pl.semaphore_wait(barrier, len(others) + n_level * (low + high))
+    tell(0)
     send_out(0)
     for q in others:
         peer_copy(0, q, lv).start()
-    for q, level in row:
-        pl.semaphore_signal(column_in, inc=1, device_id={"space": q, "level": level})
     for i in range(len(loads)):
         if i not in early:
             loads[i].wait()
@@ -478,25 +509,33 @@
     adjoint_sum[...] = jnp.zeros((8, 2 * LANES), jnp.float32)
     listed_tables()
 
+    each = -(-(rounds - 1) // (STEPS - 1))
+
     def step(s, _):
-        @pl.when(s == STEPS - 1)
-        def _():
-            start_volume()
-
         own_parts()
 
         @pl.when(s < 2)
         def _():
             make_adjoint(s)
+
+        for turn in range(STEPS - 1):
+            @pl.when(s == turn)
+            def _():
+                for j in range(turn * each, min((turn + 1) * each, rounds - 1)):
+                    hear(j)
+                    tell(j + 1)
+
+        @pl.when(s == STEPS - 2)
+        def _():
+            add_early()
 
         for q in others:
             peer_copy(s, q, q).wait_recv()
         own_surface(s)
         receive(s)
-
         close(s)
 
-        @pl.when(s < STEPS - 1)
+        @pl.when(s < STEPS - 2)
         def _():
             finish_listed(s)
             send_out(s + 1)
@@ -504,6 +543,13 @@
         finish(s)
         for q in others:
             peer_copy(s + 1, q, lv).start()
+
+        @pl.when(s == STEPS - 2)
+        def _():
+            start_late()
+            finish_listed(s)
+            send_out(s + 1)
+
         return 0
 
     lax.fori_loop(0, STEPS, step, 0)
@@ -525,11 +571,17 @@
         def _():
             adjoint_copy(side).wait_send()
 
-    vol_every().wait_send()
-    vol_every().wait_recv()
-    total = lax.fori_loop(0, n_dev - 1, lambda d, total: total + vol_all[d], vol_line[...], unroll=n_dev <= 64)
-    drifts = total / total[:, STEPS:STEPS + 1]
-    shift = jnp.sum(jnp.where(lane_ids < STEPS, drifts, 0.0), axis=1, keepdims=True)
+    every_line().wait_send()
+    every_line().wait_recv()
+    total = add_lines()
+    early = total[:1]
+    area_total = early[:, STEPS:STEPS + 1]
+    drifts = early / area_total
+    shift = jnp.sum(jnp.where(lane_ids < STEPS - 2, drifts, 0.0), axis=1, keepdims=True)
+    last = jnp.sum(total[1:], axis=1, keepdims=True) / area_total
+    for i in range(2):
+        drifts = jnp.where(lane_ids == STEPS - 2 + i, last[i:i + 1], drifts)
+        shift = shift + last[i:i + 1]
     ele_out[...] = level + time_step * shift
     drift_out[...] = drifts
 
@@ -544,7 +596,6 @@
 def solution(mesh):
     n_space, n_level = mesh.shape["space"], mesh.shape["level"]
     n_dev = n_space * n_level
-    width = max(w for w in range(1, n_space + 1) if n_space % w == 0 and w * w <= n_space)
 
     def local(velocity, density, elevation, grad_weights, lap_weights, coriolis,
               node_area, thickness, send_list, neighbours, bottom):
@@ -565,7 +616,7 @@
                   neighbours, bottom.reshape(plane)]
         arrays = [pltpu.with_memory_space_constraint(a, pltpu.HBM) for a in arrays]
         out = pl.pallas_call(
-            functools.partial(kernel, n_space, n_level, width, rows, blocks, near_count),
+            functools.partial(kernel, n_space, n_level, rows, blocks, near_count),
             out_shape=(
                 jax.ShapeDtypeStruct(velocity.shape, f32),
                 jax.ShapeDtypeStruct(density.shape, f32),
@@ -601,9 +652,11 @@
                 pltpu.VMEM((STEPS, 2, n_level, 1, LANES), f32),
                 pltpu.VMEM((STEPS + 1, 2) + plane, f32),
                 pltpu.VMEM((STEPS + 1, n_level) + plane, f32),
+                pltpu.VMEM((blocks,) + pack, f32),
                 pltpu.VMEM(pack, f32),
                 pltpu.VMEM((1, LANES), f32),
-                pltpu.VMEM((n_dev - 1, 1, LANES), f32),
+                pltpu.VMEM((3, LANES), f32),
+                pltpu.VMEM((n_dev - 1, 3, LANES), f32),
                 pltpu.VMEM((8, 2 * LANES), f32),
                 pltpu.VMEM((2,) + pack, f32),
                 pltpu.VMEM((2,) + pack, f32),
@@ -612,7 +665,7 @@
                 dma((n_level,)), dma((2, n_level)),
                 dma, dma,
                 dma((2,)), dma((2,)),
-                pltpu.SemaphoreType.REGULAR,
+                pltpu.SemaphoreType.REGULAR(((n_space - 1).bit_length(),)),
                 dma((11,)),
                 pltpu.SMEM(thickness.shape, f32),
             ] + [pltpu.VMEM(a.shape, a.dtype) for a in arrays[:7] + arrays[8:]],

time: 24.2 us -> 23.9 us (0.988)
  Pallas kernels: 23.4 us -> 23.1 us
    pallas_call x1, Pallas kernels: 22.8 us -> 22.5 us  [local(): pl.pallas_call(functools.partial(kernel, n_space, n_level, rows, blocks,...]
where the time goes in v3:
time: 23.9 us; the launch traced here: 23.7 us
  Pallas kernels  23.1 us (97%)
  between operations  0.64 us (3%)
    pallas_call x1, Pallas kernels, local(): pl.pallas_call(functools.partial(kernel, n_space, n_level, rows, blocks,...  22.5 us
    pallas_call x1, Pallas kernels, local(): pl.pallas_call(emit, out_shape=(jax.ShapeDtypeStruct(velocity.shape, f32)...  0.65 us

profile of v3, /device:TPU:0, one launch (start us, length us, event | category | flops | bytes accessed | tf_op | source)
XLA Modules:
  0.0 23.7 jit_solution(14049331671493885951)
XLA Ops:
  0.6 22.5 %shard_map.138 = (f32[2,8,1024]{2,1,0:T(8,128)S(1)}, f32[8,1024]{1,0:T(8,128)S(1)}, f32[8,128]{1,0:T(8,128)S(1)}, f32[1,128]{1,0:T(1,128)S(1)}) custom-call(f32[2,8,1024]{2,1,0:T(8,128)} %vel.1, f32[8,1024]{1,0:T(8,128)} %den.1, f32[8,128]{1,0:T(8,128)} %bitcast.8, f32[6,2,1024]{2,1,0:T(2,128)} %bitcast.7, f32[6,1024]{1,0:T(8,128)} %lap.1, ...), custom_call_target="tpu_custom_call" | custom-call | tf_op jit(solution)/shard_map/pallas_call | solution.py:618
  23.1 0.6 %shard_map.139 = (f32[2,8,1024]{2,1,0:T(8,128)}, f32[8,1024]{1,0:T(8,128)}, f32[8,128]{1,0:T(8,128)}, f32[1,4]{1,0:T(1,128)}) custom-call(f32[2,8,1024]{2,1,0:T(8,128)S(1)} %get-tuple-element.12.vel, f32[8,1024]{1,0:T(8,128)S(1)} %get-tuple-element.13.den, f32[8,128]{1,0:T(8,128)S(1)} %get-tuple-element.14.ele, f32[1,128]{1,0:T(1,128)S(1)} %get-tuple-element.15.drift), custom_call_target="tpu_custom_call" | custom-call | tf_op jit(solution)/shard_map/pallas_call | solution.py:675

commit v4 on v3

--- a/solution.py
+++ b/solution.py
@@ -44,13 +44,13 @@
 
 
 def kernel(
-    n_space, n_level, rows, blocks, near_count,
+    n_space, n_level, width, rows, blocks, near_count,
     vel, den, ele, grad, lap, cor, area, thick, send, near, bot,
     vel_out, den_out, ele_out, drift_out,
     own, eta, cor_of, bot_of, lanes_of, block_of, weight_of, pack_lanes, pack_block, pack_weight,
     flow_lanes, flow_block, flow_own, flow_halo,
     part, q_part, q_of, q_edge, q_sum, small, out, out_small, halo, halo_small, peer_out, peer,
-    flow, vol, vol_line, line, lines, adjoint_sum, adjoint, adjoint_in,
+    flow, vol, line, lines, adjoint_sum, adjoint, adjoint_in,
     main_send, main_recv, hs_send, hs_recv, peer_send, peer_recv, line_send, line_recv, adj_send, adj_recv, ready,
     load_sem, thick_in, *loaded,
 ):
@@ -64,6 +64,8 @@
     high = jnp.where(has[1], 1, 0)
     others = [lax.rem(lv + d, n_level) for d in range(1, n_level)]
     targets = blocks + 2
+    far = jnp.where(lax.rem(sp, width) == 0, 0, 1)
+    near_side = 1 - far
 
     barrier = pltpu.get_barrier_semaphore()
 
@@ -130,7 +132,7 @@
         cor_of[t] = turn
         lane_pack = jnp.zeros((8, LANES), jnp.int32)
         block_pack = bottom[:8]
-        packs = [jnp.zeros((8, LANES), jnp.float32) for _ in range(6)]
+        packs = [jnp.zeros((8, LANES), jnp.float32) for _ in range(9)]
         packs[2] = turn[:8]
         flows = [[jnp.zeros((8, LANES), jnp.int32)] * 2 + [jnp.zeros((8, LANES), jnp.float32)] * 2
                  for _ in range(flow_own.shape[1])]
@@ -139,12 +141,13 @@
             block = lax.shift_right_logical(slot, 7)
             lanes = jnp.bitwise_and(slot, LANES - 1)
             inside = block < blocks
-            outside = jnp.where(inside, 0, jnp.where(block == blocks, low, high)) > 0
+            below = jnp.where(block == blocks, low, 0) > 0
+            above = jnp.where(block == blocks + 1, high, 0) > 0
             lanes_of[t, k] = lanes
             block_of[t, k] = block
             values = (wide(grad[k, 0:1, here]), wide(grad[k, 1:2, here]), wide(lap[k:k + 1, here]))
-            picked = [jnp.where(mask, value, 0.0) for mask in (inside, outside) for value in values]
-            for i in range(6):
+            picked = [jnp.where(mask, value, 0.0) for mask in (inside, below, above) for value in values]
+            for i in range(9):
                 weight_of[t, k, i] = picked[i]
             mine = eight == k
             lane_pack = jnp.where(mine, lanes[:8], lane_pack)
@@ -156,10 +159,10 @@
             flow[0] = jnp.where(pair, lanes[:8], flow[0])
             flow[1] = jnp.where(pair, block[:8], flow[1])
             flow[2] = jnp.where(pair, jnp.where(odd, picked[1][:8], picked[0][:8]), flow[2])
-            flow[3] = jnp.where(pair, jnp.where(odd, picked[4][:8], picked[3][:8]), flow[3])
+            flow[3] = jnp.where(pair, jnp.where(odd, (picked[4] + picked[7])[:8], (picked[3] + picked[6])[:8]), flow[3])
         pack_lanes[t] = lane_pack
         pack_block[t] = block_pack
-        for i in range(6):
+        for i in range(9):
             pack_weight[t, i] = packs[i]
         for j in range(flow_own.shape[1]):
             flow_lanes[t, j], flow_block[t, j], flow_own[t, j], flow_halo[t, j] = flows[j]
@@ -178,17 +181,17 @@
             lanes, masks = lanes[:8], [mask[:8] for mask in masks]
             found_lanes = pick([pack_lanes[b] for b in range(blocks)], lanes, masks)
             found_block = pick([pack_block[b] for b in range(blocks)], lanes, masks)
-            found = [pick([pack_weight[b, i] for b in range(blocks)], lanes, masks) for i in range(6)]
+            found = [pick([pack_weight[b, i] for b in range(blocks)], lanes, masks) for i in range(9)]
             pack_lanes[t] = found_lanes
             pack_block[t] = found_block
-            for i in range(6):
+            for i in range(9):
                 pack_weight[t, i] = found[i]
             bot_of[t] = wide(found_block[7:8])
             cor_of[t] = wide(found[2][7:8])
             for k in range(near_count):
                 lanes_of[t, k] = wide(found_lanes[k:k + 1])
                 block_of[t, k] = wide(found_block[k:k + 1])
-                for i in range(6):
+                for i in range(9):
                     weight_of[t, k, i] = wide(found[i][k:k + 1])
 
     def version(q):
@@ -205,6 +208,18 @@
             src_ref=out_small.at[s, side, version(q)], dst_ref=halo_small.at[s, 1 - side, slot],
             send_sem=hs_send.at[side, q], recv_sem=hs_recv.at[lax.rem(s, 2), 1 - side, slot],
             device_id={"space": ends[side], "level": q}, device_id_type=pl.DeviceIdType.MESH)
+
+    def main_wait(s, side):
+        return pltpu.make_async_remote_copy(
+            src_ref=out.at[s, side], dst_ref=halo.at[s, side],
+            send_sem=main_send.at[side], recv_sem=main_recv.at[lax.rem(s, 2), side],
+            device_id={"space": sp - 1 + 2 * side, "level": lv}, device_id_type=pl.DeviceIdType.MESH)
+
+    def small_wait(s, side, q):
+        return pltpu.make_async_remote_copy(
+            src_ref=out_small.at[s, side, 0], dst_ref=halo_small.at[s, side, q],
+            send_sem=hs_send.at[side, q], recv_sem=hs_recv.at[lax.rem(s, 2), side, q],
+            device_id={"space": sp - 1 + 2 * side, "level": q}, device_id_type=pl.DeviceIdType.MESH)
 
     def adjoint_copy(side):
         return pltpu.make_async_remote_copy(
@@ -337,35 +352,61 @@
             q_part[t, 0] = pack_weight[t, 0] * diff
             q_part[t, 1] = pack_weight[t, 1] * diff
 
-    def receive(s):
-        for side in range(2):
-            @pl.when(has[side])
-            def _():
-                main_copy(s, 1 - side).wait_recv()
-                for q in others:
-                    small_copy(s, 1 - side, q, q).wait_recv()
-        for side in range(2):
-            total = halo[s, side, 3 * rows:3 * rows + 1]
+    def receive(s, side):
+        @pl.when(jnp.where(side == 0, low, high) > 0)
+        def _():
+            main_wait(s, side).wait_recv()
             for q in others:
-                total = total + halo_small[s, side, q]
-            q_edge[side] = wide(total, 8)
-
-    def advance(s, t):
-        edges = [[halo[s, side, g * rows:(g + 1) * rows] for side in range(2)] for g in range(3)]
+                small_wait(s, side, q).wait_recv()
+
+        total = halo[s, side, 3 * rows:3 * rows + 1]
+        for q in others:
+            total = total + halo_small[s, side, q]
+        return wide(total, 8)
+
+    def edge_sums(s, side, t, sums):
         here = [own[g, t] for g in range(3)]
-        sums = [part[t, i] for i in range(6)]
+        edge = [halo[s, side, g * rows:(g + 1) * rows] for g in range(3)]
         for k in range(near_count):
             lanes = lanes_of[t, k]
-            upper = block_of[t, k] == blocks + 1
-            diff = [jnp.where(upper, lane_gather(edges[g][1], lanes), lane_gather(edges[g][0], lanes)) - here[g]
-                    for g in range(3)]
-            sums = gathered(sums, diff, [weight_of[t, k, 3 + i] for i in range(3)])
+            diff = [lane_gather(edge[g], lanes) - here[g] for g in range(3)]
+            sums = gathered(sums, diff, [weight_of[t, k, 3 + 3 * side + i] for i in range(3)])
+        return sums
+
+    def edge_surface(side, edge, t):
+        diff = lane_gather(edge, pack_lanes[t]) - q_of[t]
+        return [q_part[t, i] + pack_weight[t, 3 + 3 * side + i] * diff for i in range(2)]
+
+    def near_part(s, t):
+        sums = edge_sums(s, near_side, t, [part[t, i] for i in range(6)])
+        for i in range(6):
+            part[t, i] = sums[i]
+        slopes = edge_surface(near_side, q_edge[1], t)
+        for i in range(2):
+            q_part[t, i] = slopes[i]
+
+    def near_listed(s):
+        for side in range(2):
+            near_part(s, blocks + side)
+
+    def near_own(s):
+        several = max(d for d in (1, 2, 4) if blocks % d == 0)
+
+        def bodies(i, _):
+            for j in range(several):
+                near_part(s, i * several + j)
+            return 0
+        lax.fori_loop(0, blocks // several, bodies, 0)
+
+    def advance(s, t, both=False):
+        here = [own[g, t] for g in range(3)]
+        sums = edge_sums(s, far, t, [part[t, i] for i in range(6)])
+        slopes = edge_surface(far, q_edge[0], t)
+        if both:
+            sums = edge_sums(s, near_side, t, sums)
+            slopes = [a + b - q_part[t, i] for i, (a, b) in enumerate(zip(slopes, edge_surface(near_side, q_edge[1], t)))]
         lap0, lap1, lap2, east2, north2, flow = sums
-        lanes = pack_lanes[t]
-        diff = jnp.where(pack_block[t] == blocks + 1, lane_gather(q_edge[1], lanes),
-                         lane_gather(q_edge[0], lanes)) - q_of[t]
-        slope0 = spread_sum(q_part[t, 0] + pack_weight[t, 3] * diff)
-        slope1 = spread_sum(q_part[t, 1] + pack_weight[t, 4] * diff)
+        slope0, slope1 = [spread_sum(slope) for slope in slopes]
         bottom, turn = bot_of[t], cor_of[t]
         drag = jnp.where(level_ids == bottom - 1, drag_rate, 0.0)
         u, v, rho = here
@@ -389,10 +430,10 @@
             fields, _, level, heavy = advance(s, blocks + side)
             stage(s + 1, side, fields, level, heavy)
 
-    def finish(s):
+    def finish(s, both=False):
         def body(t, carry):
             volume, light, heavy = carry
-            fields, diverge, level, more = advance(s, t)
+            fields, diverge, level, more = advance(s, t, both)
             for g in range(3):
                 own[g, t] = fields[g]
             flow[t] = transport(fields)
@@ -415,7 +456,8 @@
                 slot = jnp.maximum((block_of[t, k][:1] - blocks) * LANES + lanes_of[t, k][:1], -1)
                 slot = jnp.broadcast_to(slot.astype(jnp.bfloat16), ids.shape)
                 hot = jnp.where(ids == slot, jnp.bfloat16(1), jnp.bfloat16(0))
-                value = jnp.where(odd, weight_of[t, k, 4][:8], weight_of[t, k, 3][:8]) * weight
+                value = jnp.where(odd, (weight_of[t, k, 4] + weight_of[t, k, 7])[:8],
+                                  (weight_of[t, k, 3] + weight_of[t, k, 6])[:8]) * weight
                 high = value.astype(jnp.bfloat16).astype(jnp.float32)
                 value = value - high
                 middle = value.astype(jnp.bfloat16).astype(jnp.float32)
@@ -425,9 +467,16 @@
                     value.astype(jnp.bfloat16), hot, (((1,), (1,)), ((), ())), preferred_element_type=jnp.float32)
             return total
 
-        half = -(-blocks // 2)
-        total = lax.fori_loop(s * half, jnp.minimum((s + 1) * half, blocks), body, adjoint_sum[...])
-        adjoint_sum[...] = total
+        cut = 3 * blocks // 4
+        for turn, spread in ((0, range(cut)), (1, range(cut, blocks))):
+            @pl.when(s == turn)
+            def _():
+                total = adjoint_sum[...]
+                for t in spread:
+                    total = body(t, total)
+                adjoint_sum[...] = total
+
+        total = adjoint_sum[...]
         total = total + pltpu.roll(total, 4, 0)
         total = total + pltpu.roll(total, 2, 0)
         for side in range(2):
@@ -435,13 +484,6 @@
             @pl.when(jnp.logical_and(has[side], s == 1))
             def _():
                 adjoint_copy(side).start()
-
-    def add_early():
-        sums = jnp.sum(vol[...], axis=1, keepdims=True)
-        total = jnp.zeros((1, LANES), jnp.float32)
-        for i in (*range(STEPS - 2), STEPS):
-            total = jnp.where(lane_ids == i, sums[i:i + 1], total)
-        vol_line[...] = total
 
     def start_late():
         for side in range(2):
@@ -461,8 +503,11 @@
             lanes, masks = listed(side)
             found = pick(tiles, lanes[:8], [mask[:8] for mask in masks])
             volume = volume + jnp.where(eight < 2, adjoint_in[side] * found, 0.0)
-        volume = jnp.where(eight == 1, vol[...][STEPS - 2:STEPS - 1], spread_sum(volume))
-        line[...] = jnp.where(eight == 0, vol_line[...], volume)[:3]
+        sums = jnp.sum(jnp.where(eight == STEPS - 1, spread_sum(volume), vol[...]), axis=1, keepdims=True)
+        total = jnp.zeros((1, LANES), jnp.float32)
+        for i in range(STEPS + 1):
+            total = jnp.where(lane_ids == i, sums[i:i + 1], total)
+        line[...] = total
         hear(rounds - 1)
         send_lines()
 
@@ -493,11 +538,6 @@
         found = pick([small[b] for b in range(blocks)], lanes[:8], [m[:8] for m in masks])
         stage(0, side, fields, wide(found[:1], 8), wide(found[1:2], 8))
 
-    pl.semaphore_wait(barrier, len(others) + n_level * (low + high))
-    tell(0)
-    send_out(0)
-    for q in others:
-        peer_copy(0, q, lv).start()
     for i in range(len(loads)):
         if i not in early:
             loads[i].wait()
@@ -509,6 +549,11 @@
     adjoint_sum[...] = jnp.zeros((8, 2 * LANES), jnp.float32)
     listed_tables()
 
+    pl.semaphore_wait(barrier, len(others) + n_level * (low + high))
+    tell(0)
+    send_out(0)
+    for q in others:
+        peer_copy(0, q, lv).start()
     each = -(-(rounds - 1) // (STEPS - 1))
 
     def step(s, _):
@@ -525,22 +570,35 @@
                     hear(j)
                     tell(j + 1)
 
-        @pl.when(s == STEPS - 2)
-        def _():
-            add_early()
-
         for q in others:
             peer_copy(s, q, q).wait_recv()
         own_surface(s)
-        receive(s)
+        q_edge[1] = receive(s, near_side)
+
+        @pl.when(s < STEPS - 1)
+        def _():
+            near_listed(s)
+
+        @pl.when(s >= STEPS - 2)
+        def _():
+            near_own(s)
+
         close(s)
+        q_edge[0] = receive(s, far)
 
         @pl.when(s < STEPS - 2)
         def _():
             finish_listed(s)
             send_out(s + 1)
 
-        finish(s)
+        @pl.when(s < STEPS - 2)
+        def _():
+            finish(s, True)
+
+        @pl.when(s >= STEPS - 2)
+        def _():
+            finish(s)
+
         for q in others:
             peer_copy(s + 1, q, lv).start()
 
@@ -574,14 +632,8 @@
     every_line().wait_send()
     every_line().wait_recv()
     total = add_lines()
-    early = total[:1]
-    area_total = early[:, STEPS:STEPS + 1]
-    drifts = early / area_total
-    shift = jnp.sum(jnp.where(lane_ids < STEPS - 2, drifts, 0.0), axis=1, keepdims=True)
-    last = jnp.sum(total[1:], axis=1, keepdims=True) / area_total
-    for i in range(2):
-        drifts = jnp.where(lane_ids == STEPS - 2 + i, last[i:i + 1], drifts)
-        shift = shift + last[i:i + 1]
+    drifts = total / total[:, STEPS:STEPS + 1]
+    shift = jnp.sum(jnp.where(lane_ids < STEPS, drifts, 0.0), axis=1, keepdims=True)
     ele_out[...] = level + time_step * shift
     drift_out[...] = drifts
 
@@ -596,13 +648,14 @@
 def solution(mesh):
     n_space, n_level = mesh.shape["space"], mesh.shape["level"]
     n_dev = n_space * n_level
+    width = max(w for w in range(1, n_space + 1) if n_space % w == 0 and w * w <= n_space)
 
     def local(velocity, density, elevation, grad_weights, lap_weights, coriolis,
               node_area, thickness, send_list, neighbours, bottom):
         rows, nodes = density.shape
         blocks = nodes // LANES
         near_count = neighbours.shape[0]
-        assert near_count < 8 and rows == 8
+        assert near_count < 8 and rows == 8 and blocks % 2 == 0
         packs = -(-near_count // 4)
         f32, i32 = jnp.float32, jnp.int32
         plane = (blocks, LANES)
@@ -616,7 +669,7 @@
                   neighbours, bottom.reshape(plane)]
         arrays = [pltpu.with_memory_space_constraint(a, pltpu.HBM) for a in arrays]
         out = pl.pallas_call(
-            functools.partial(kernel, n_space, n_level, rows, blocks, near_count),
+            functools.partial(kernel, n_space, n_level, width, rows, blocks, near_count),
             out_shape=(
                 jax.ShapeDtypeStruct(velocity.shape, f32),
                 jax.ShapeDtypeStruct(density.shape, f32),
@@ -632,10 +685,10 @@
                 pltpu.VMEM((blocks + 2,) + tile, i32),
                 pltpu.VMEM((blocks + 2, near_count) + tile, i32),
                 pltpu.VMEM((blocks + 2, near_count) + tile, i32),
-                pltpu.VMEM((blocks + 2, near_count, 6) + tile, f32),
+                pltpu.VMEM((blocks + 2, near_count, 9) + tile, f32),
                 pltpu.VMEM((blocks + 2,) + pack, i32),
                 pltpu.VMEM((blocks + 2,) + pack, i32),
-                pltpu.VMEM((blocks + 2, 6) + pack, f32),
+                pltpu.VMEM((blocks + 2, 9) + pack, f32),
                 pltpu.VMEM((blocks, packs) + pack, i32),
                 pltpu.VMEM((blocks, packs) + pack, i32),
                 pltpu.VMEM((blocks, packs) + pack, f32),
@@ -655,8 +708,7 @@
                 pltpu.VMEM((blocks,) + pack, f32),
                 pltpu.VMEM(pack, f32),
                 pltpu.VMEM((1, LANES), f32),
-                pltpu.VMEM((3, LANES), f32),
-                pltpu.VMEM((n_dev - 1, 3, LANES), f32),
+                pltpu.VMEM((n_dev - 1, 1, LANES), f32),
                 pltpu.VMEM((8, 2 * LANES), f32),
                 pltpu.VMEM((2,) + pack, f32),
                 pltpu.VMEM((2,) + pack, f32),

time: 23.9 us -> 23.6 us (0.987)
  Pallas kernels: 23.1 us -> 22.8 us
    pallas_call x1, Pallas kernels: 22.5 us -> 22.1 us  [local(): pl.pallas_call(functools.partial(kernel, n_space, n_level, width, rows, b...]
where the time goes in v4:
time: 23.6 us; the launch traced here: 23.4 us
  Pallas kernels  22.8 us (97%)
  between operations  0.64 us (3%)
    pallas_call x1, Pallas kernels, local(): pl.pallas_call(functools.partial(kernel, n_space, n_level, width, rows, b...  22.1 us
    pallas_call x1, Pallas kernels, local(): pl.pallas_call(emit, out_shape=(jax.ShapeDtypeStruct(velocity.shape, f32)...  0.65 us

profile of v4, /device:TPU:0, one launch (start us, length us, event | category | flops | bytes accessed | tf_op | source)
XLA Modules:
  0.0 23.4 jit_solution(1399108541338968908)
XLA Ops:
  0.6 22.1 %shard_map.138 = (f32[2,8,1024]{2,1,0:T(8,128)S(1)}, f32[8,1024]{1,0:T(8,128)S(1)}, f32[8,128]{1,0:T(8,128)S(1)}, f32[1,128]{1,0:T(1,128)S(1)}) custom-call(f32[2,8,1024]{2,1,0:T(8,128)} %vel.1, f32[8,1024]{1,0:T(8,128)} %den.1, f32[8,128]{1,0:T(8,128)} %bitcast.8, f32[6,2,1024]{2,1,0:T(2,128)} %bitcast.7, f32[6,1024]{1,0:T(8,128)} %lap.1, ...), custom_call_target="tpu_custom_call" | custom-call | tf_op jit(solution)/shard_map/pallas_call | solution.py:671
  22.8 0.6 %shard_map.139 = (f32[2,8,1024]{2,1,0:T(8,128)}, f32[8,1024]{1,0:T(8,128)}, f32[8,128]{1,0:T(8,128)}, f32[1,4]{1,0:T(1,128)}) custom-call(f32[2,8,1024]{2,1,0:T(8,128)S(1)} %get-tuple-element.12.vel, f32[8,1024]{1,0:T(8,128)S(1)} %get-tuple-element.13.den, f32[8,128]{1,0:T(8,128)S(1)} %get-tuple-element.14.ele, f32[1,128]{1,0:T(1,128)S(1)} %get-tuple-element.15.drift), custom_call_target="tpu_custom_call" | custom-call | tf_op jit(solution)/shard_map/pallas_call | solution.py:727

commit v5 on v4

--- a/solution.py
+++ b/solution.py
@@ -286,7 +286,6 @@
             own[g, blocks + side] = fields[g]
             out[s, side, g * rows:(g + 1) * rows] = fields[g]
         eta[blocks + side] = level
-        out[s, side, 3 * rows:3 * rows + 8] = level
         out_small[s, side, 0] = level[:1]
         out_small[s, side, 1] = heavy[:1]
 
@@ -295,7 +294,7 @@
             @pl.when(has[side])
             def _():
                 main_copy(s, side).start()
-                for q in others:
+                for q in [lv] + others:
                     small_copy(s, side, q, lv).start()
 
     def close(s):
@@ -305,7 +304,7 @@
             @pl.when(has[side])
             def _():
                 main_copy(s, side).wait_send()
-                for q in others:
+                for q in [lv] + others:
                     small_copy(s, side, q, lv).wait_send()
 
     def gathered(sums, diff, weights):
@@ -356,10 +355,10 @@
         @pl.when(jnp.where(side == 0, low, high) > 0)
         def _():
             main_wait(s, side).wait_recv()
-            for q in others:
+            for q in [lv] + others:
                 small_wait(s, side, q).wait_recv()
 
-        total = halo[s, side, 3 * rows:3 * rows + 1]
+        total = halo_small[s, side, lv]
         for q in others:
             total = total + halo_small[s, side, q]
         return wide(total, 8)
@@ -699,9 +698,9 @@
                 pltpu.VMEM((2,) + pack, f32),
                 pltpu.VMEM(plane, f32),
                 pltpu.VMEM((blocks,) + pack, f32),
-                pltpu.VMEM((STEPS, 2, 3 * rows + 8, LANES), f32),
+                pltpu.VMEM((STEPS, 2, 3 * rows, LANES), f32),
                 pltpu.VMEM((STEPS, 2, 2, 1, LANES), f32),
-                pltpu.VMEM((STEPS, 2, 3 * rows + 8, LANES), f32),
+                pltpu.VMEM((STEPS, 2, 3 * rows, LANES), f32),
                 pltpu.VMEM((STEPS, 2, n_level, 1, LANES), f32),
                 pltpu.VMEM((STEPS + 1, 2) + plane, f32),
                 pltpu.VMEM((STEPS + 1, n_level) + plane, f32),

time: 23.6 us -> 23.7 us (level)
  no operation moved by 1% of the time
where the time goes in v5:
time: 23.7 us; the launch traced here: 23.6 us
  Pallas kernels  22.9 us (97%)
  between operations  0.64 us (3%)
    pallas_call x1, Pallas kernels, local(): pl.pallas_call(functools.partial(kernel, n_space, n_level, width, rows, b...  22.3 us
    pallas_call x1, Pallas kernels, local(): pl.pallas_call(emit, out_shape=(jax.ShapeDtypeStruct(velocity.shape, f32)...  0.65 us

profile of v5, /device:TPU:0, one launch (start us, length us, event | category | flops | bytes accessed | tf_op | source)
XLA Modules:
  0.0 23.6 jit_solution(5871520846466992318)
XLA Ops:
  0.6 22.3 %shard_map.138 = (f32[2,8,1024]{2,1,0:T(8,128)S(1)}, f32[8,1024]{1,0:T(8,128)S(1)}, f32[8,128]{1,0:T(8,128)S(1)}, f32[1,128]{1,0:T(1,128)S(1)}) custom-call(f32[2,8,1024]{2,1,0:T(8,128)} %vel.1, f32[8,1024]{1,0:T(8,128)} %den.1, f32[8,128]{1,0:T(8,128)} %bitcast.8, f32[6,2,1024]{2,1,0:T(2,128)} %bitcast.7, f32[6,1024]{1,0:T(8,128)} %lap.1, ...), custom_call_target="tpu_custom_call" | custom-call | tf_op jit(solution)/shard_map/pallas_call | solution.py:670
  22.9 0.6 %shard_map.139 = (f32[2,8,1024]{2,1,0:T(8,128)}, f32[8,1024]{1,0:T(8,128)}, f32[8,128]{1,0:T(8,128)}, f32[1,4]{1,0:T(1,128)}) custom-call(f32[2,8,1024]{2,1,0:T(8,128)S(1)} %get-tuple-element.12.vel, f32[8,1024]{1,0:T(8,128)S(1)} %get-tuple-element.13.den, f32[8,128]{1,0:T(8,128)S(1)} %get-tuple-element.14.ele, f32[1,128]{1,0:T(1,128)S(1)} %get-tuple-element.15.drift), custom_call_target="tpu_custom_call" | custom-call | tf_op jit(solution)/shard_map/pallas_call | solution.py:726
